TPU v7x, 8 devices: a whole 2x2x1 slice. The times are simulated.
8 devices in a mesh: dp: 1 (over z), pp: 2 (over y), tp: 4 (over x, core).
Axes of the slice: x: 2, y: 2, z: 1, core: 2. Of those that a mesh axis runs over, the one named last changes fastest.
Arguments:
- x_in: bfloat16 [8, 512, 6144], P('dp')
- seq_len: int32 [8], P('dp')
- norm_attn: bfloat16 [2, 6144], P('pp')
- w_qa: bfloat16 [2, 6144, 1536], P('pp')
- norm_q: bfloat16 [2, 1536], P('pp')
- w_qb: bfloat16 [2, 1536, 12288], P('pp', None, 'tp')
- w_kva: bfloat16 [2, 6144, 576], P('pp')
- norm_kv: bfloat16 [2, 512], P('pp')
- w_kvb: bfloat16 [2, 512, 16384], P('pp', None, 'tp')
- w_o: bfloat16 [2, 8192, 6144], P('pp', 'tp')
- norm_mlp: bfloat16 [2, 6144], P('pp')
- w_gate: bfloat16 [2, 6144, 12288], P('pp', None, 'tp')
- w_up: bfloat16 [2, 6144, 12288], P('pp', None, 'tp')
- w_down: bfloat16 [2, 12288, 6144], P('pp', 'tp')
- norm_final: bfloat16 [6144], replicated
Outputs:
- output 1: bfloat16 [2, 8, 512, 512], P('pp', 'dp')
- output 2: bfloat16 [2, 8, 512, 64], P('pp', 'dp')
- output 3: bfloat16 [8, 6144], P('dp')
All inputs are finite; a program needn't handle non-finite values.
Results may differ from a plain program's by a relative error of at most 0.0180411.
Values are sent between devices in bfloat16 or wider.
A program may use at most 1 GiB of HBM per device.

v0:
```python
import math
import jax
import jax.numpy as jnp
from jax import lax
from jax.sharding import PartitionSpec as P

RMS_EPS = 1e-5
ROPE_BASE = 10000.0
SCALE_DEPTH = 1.4


def rms_norm(values_in, gain):
    wide_vals = values_in.astype(jnp.float32)
    inv_rms = lax.rsqrt(jnp.mean(wide_vals * wide_vals, axis=-1, keepdims=True) + RMS_EPS)
    return (wide_vals * inv_rms * gain.astype(jnp.float32)).astype(jnp.bfloat16)


def rope_tables(seq_size, rope_dim):
    half_dim = rope_dim // 2
    inv_freq = ROPE_BASE ** (-2.0 * jnp.arange(half_dim, dtype=jnp.float32) / rope_dim)
    angle = jnp.arange(seq_size, dtype=jnp.float32)[:, None] * inv_freq[None, :]
    return jnp.cos(angle), jnp.sin(angle)


def apply_rope(values_in, cos_t, sin_t):
    half_dim = values_in.shape[-1] // 2
    wide_vals = values_in.astype(jnp.float32)
    lo_half = wide_vals[..., :half_dim]
    hi_half = wide_vals[..., half_dim:]
    return jnp.concatenate([lo_half * cos_t - hi_half * sin_t, hi_half * cos_t + lo_half * sin_t], axis=-1).astype(jnp.bfloat16)


def head_dims(wq_up, wkv_up, wo_any, wkv_down, g_kv):
    rope_dim = wkv_down.shape[-1] - g_kv.shape[-1]
    heads = (wq_up.shape[-1] - wkv_up.shape[-1] + wo_any.shape[-2]) // rope_dim
    return heads, (wkv_up.shape[-1] - wo_any.shape[-2]) // heads, rope_dim, wo_any.shape[-2] // heads


def matmul_f32(act_in, weight):
    return jnp.dot(act_in, weight, preferred_element_type=jnp.float32)


def residual(hidden, branch, res_scale):
    return (hidden.astype(jnp.float32) + res_scale * branch.astype(jnp.float32)).astype(jnp.bfloat16)


def attend(q_nope, q_rope, k_nope, k_rope, values, lens):
    seq_size = q_nope.shape[1]
    positions = jnp.arange(seq_size)
    score_scale = (q_nope.shape[-1] + q_rope.shape[-1]) ** -0.5
    scores = (jnp.einsum("bshd,bthd->bhst", q_nope, k_nope, preferred_element_type=jnp.float32)
              + jnp.einsum("bshd,btd->bhst", q_rope, k_rope, preferred_element_type=jnp.float32)) * score_scale
    allowed = (positions[:, None] >= positions[None, :])[None, None] & (positions[None, None, None, :] < lens[:, None, None, None])
    attn_probs = jax.nn.softmax(jnp.where(allowed, scores, -1e30), axis=-1).astype(jnp.bfloat16)
    return jnp.einsum("bhst,bthd->bshd", attn_probs, values, preferred_element_type=jnp.float32).astype(jnp.bfloat16)


def solution(mesh):
    tp_size = mesh.shape["tp"]
    pp_size = mesh.shape["pp"]

    def layer_step(hidden, lens, weights, cos_t, sin_t, res_scale):
        g_attn, wq_down, g_q, wq_up, wkv_down, g_kv, wkv_up, wo_part, g_mlp, wgate_part, wup_part, wdown_part = weights
        micro_rows, seq_size, d_model = hidden.shape
        value_a6 = g_q.shape[-1]
        value_a7 = g_kv.shape[-1]
        heads, nope_dim, rope_dim, v_head = head_dims(wq_up, wkv_up, wo_part, wkv_down, g_kv)
        normed = rms_norm(hidden, g_attn).reshape(micro_rows * seq_size, d_model)
        share_rows = (micro_rows * seq_size) // tp_size
        my_rows = lax.dynamic_slice_in_dim(normed, lax.axis_index("tp") * share_rows, share_rows, axis=0)
        q_down = rms_norm(matmul_f32(my_rows, wq_down).astype(jnp.bfloat16), g_q)
        latent_raw = matmul_f32(my_rows, wkv_down).astype(jnp.bfloat16)
        c_kv = rms_norm(latent_raw[:, :value_a7], g_kv)
        joined = jnp.concatenate([q_down, c_kv, latent_raw[:, value_a7:]], axis=-1)
        gathered = lax.all_gather(joined, "tp", axis=0, tiled=True).reshape(micro_rows, seq_size, -1)
        q_down = gathered[..., :value_a6]
        c_kv = gathered[..., value_a6:value_a6 + value_a7]
        k_rope = apply_rope(gathered[..., value_a6 + value_a7:], cos_t, sin_t)
        q_full = matmul_f32(q_down, wq_up).astype(jnp.bfloat16).reshape(micro_rows, seq_size, heads, nope_dim + rope_dim)
        kv_full = matmul_f32(c_kv, wkv_up).astype(jnp.bfloat16).reshape(micro_rows, seq_size, heads, nope_dim + v_head)
        q_rope = apply_rope(q_full[..., nope_dim:], cos_t[:, None, :], sin_t[:, None, :])
        attn_out = attend(q_full[..., :nope_dim], q_rope, kv_full[..., :nope_dim], k_rope, kv_full[..., nope_dim:], lens)
        attn_part = matmul_f32(attn_out.reshape(micro_rows, seq_size, heads * v_head), wo_part).astype(jnp.bfloat16)
        hidden = residual(hidden, lax.psum(attn_part, "tp"), res_scale)
        normed = rms_norm(hidden, g_mlp)
        hidden_act = (jax.nn.silu(matmul_f32(normed, wgate_part)) * matmul_f32(normed, wup_part)).astype(jnp.bfloat16)
        mlp_part = matmul_f32(hidden_act, wdown_part).astype(jnp.bfloat16)
        hidden = residual(hidden, lax.psum(mlp_part, "tp"), res_scale)
        return hidden, c_kv, k_rope

    def staged(x_in, seq_len, norm_attn, w_qa, norm_q, w_qb, w_kva, norm_kv, w_kvb, w_o, norm_mlp, w_gate, w_up, w_down, norm_final):
        batch, seq_size, d_model = x_in.shape
        stage_layers = w_qa.shape[0]
        value_a7 = norm_kv.shape[-1]
        rope_dim = w_kva.shape[-1] - value_a7
        res_scale = SCALE_DEPTH / math.sqrt(stage_layers * pp_size)
        micro_rows = batch // pp_size
        cos_t, sin_t = rope_tables(seq_size, rope_dim)
        stage_idx = lax.axis_index("pp")
        micro_x = x_in.reshape(pp_size, micro_rows, seq_size, d_model)
        micro_lens = seq_len.reshape(pp_size, micro_rows)
        stacked = (norm_attn, w_qa, norm_q, w_qb, w_kva, norm_kv, w_kvb, w_o, norm_mlp, w_gate, w_up, w_down)
        shift_pairs = [(source_idx, source_idx + 1) for source_idx in range(pp_size - 1)]

        def tick_step(carry, tick_idx):
            inbox, latent_buf, rope_buf, last_buf = carry
            micro_idx = tick_idx - stage_idx
            valid = (micro_idx >= 0) & (micro_idx < pp_size)
            slot = jnp.clip(micro_idx, 0, pp_size - 1)
            hidden = jnp.where(stage_idx == 0, micro_x[slot], inbox)
            lens = micro_lens[slot]
            latents = []
            ropes = []
            for layer_idx in range(stage_layers):
                weights = tuple(stacked_arr[layer_idx] for stacked_arr in stacked)
                hidden, c_kv, k_rope = layer_step(hidden, lens, weights, cos_t, sin_t, res_scale)
                latents.append(c_kv)
                ropes.append(k_rope)
            row_start = slot * micro_rows
            new_latent = jnp.stack(latents)
            old_latent = lax.dynamic_slice_in_dim(latent_buf, row_start, micro_rows, axis=1)
            latent_buf = lax.dynamic_update_slice_in_dim(latent_buf, jnp.where(valid, new_latent, old_latent), row_start, axis=1)
            new_rope = jnp.stack(ropes)
            old_rope = lax.dynamic_slice_in_dim(rope_buf, row_start, micro_rows, axis=1)
            rope_buf = lax.dynamic_update_slice_in_dim(rope_buf, jnp.where(valid, new_rope, old_rope), row_start, axis=1)
            last_tok = jnp.take_along_axis(hidden, (lens - 1)[:, None, None], axis=1)[:, 0]
            final_rows = rms_norm(last_tok, norm_final)
            old_final = lax.dynamic_slice_in_dim(last_buf, row_start, micro_rows, axis=0)
            keep_final = valid & (stage_idx == pp_size - 1)
            last_buf = lax.dynamic_update_slice_in_dim(last_buf, jnp.where(keep_final, final_rows, old_final), row_start, axis=0)
            inbox = lax.ppermute(hidden, "pp", shift_pairs)
            return (inbox, latent_buf, rope_buf, last_buf), None

        init = (jnp.zeros((micro_rows, seq_size, d_model), jnp.bfloat16),
                jnp.zeros((stage_layers, batch, seq_size, value_a7), jnp.bfloat16),
                jnp.zeros((stage_layers, batch, seq_size, rope_dim), jnp.bfloat16),
                jnp.zeros((batch, d_model), jnp.bfloat16))
        final_carry = lax.scan(tick_step, init, jnp.arange(2 * pp_size - 1))[0]
        return final_carry[1], final_carry[2], lax.psum(final_carry[3], "pp")

    weight_specs = (P("pp", None), P("pp", None, None), P("pp", None), P("pp", None, "tp"), P("pp", None, None), P("pp", None),
                    P("pp", None, "tp"), P("pp", "tp", None), P("pp", None), P("pp", None, "tp"), P("pp", None, "tp"), P("pp", "tp", None))
    in_specs = (P("dp", None, None), P("dp")) + weight_specs + (P(None),)
    out_specs = (P("pp", "dp", None, None), P("pp", "dp", None, None), P("dp", None))
    return jax.shard_map(staged, mesh=mesh, in_specs=in_specs, out_specs=out_specs, check_vma=False)
```

profile of v0, /device:TPU:0, one launch (start us, length us, event | category | flops | bytes accessed | tf_op | source)
XLA Modules:
  0.0 6379.0 jit_solution(2475213038707129629)
XLA Ops:
  23.0 6326.7 %while.23 = (s32[]{:T(128)}, bf16[4,512,6144]{2,1,0:T(8,128)(2,1)}, bf16[1,8,512,512]{3,2,1,0:T(8,128)(2,1)}, bf16[1,8,512,64]{2,3,1,0:T(8,128)(2,1)}, bf16[8,61...) while((s32[]{:T(128)}, bf16[4,512,6144]{2,1,0:T(8,128)(2,1)}, ...), condition=%wide.region_10.11_spmd.clone.clone.clone, body=%wide.region_0.10_spmd.clone.clone.clone.sunk | while | flops 336037675008 | bytes 1639315200 | solution.py:138
  106.0 61.2 all-gather.2.cloned.1.call-done
  360.3 60.6 fusion.181
  421.7 416.5 %all-reduce.6.cloned.1.call-done = bf16[4,512,6144]{2,1,0:T(8,128)(2,1)} async-done(((bf16[4,512,6144]{2,1,0:T(8,128)(2,1)}), bf16[4,512,6144]{2,1,0:T(8,128)(2,1)}) %all-reduce.6.cloned.1.call-update) | async-done | bytes 25165840 | tf_op jit(solution)/shard_map/while/body/eval_jaxpr/psum | solution.py:84
  868.7 88.3 %fusion.184 = f32[4,512,3072]{2,1,0:T(8,128)} fusion(bf16[1,6144,3072]{2,1,0:T(8,128)(2,1)} %get-tuple-element.1043, bf16[4,512,6144]{2,1,0:T(8,128)(2,1)} %get-tuple-element.955, f32[6144]{0:T(1024)S(1)} %bitcast.167, f32[4,512]{1,0:T(4,128)S(1)} %add_rsqrt_fusion.13), kind=kOutput, calls=%fused_computation.27.clone.1 | convolution fusion | flops 77359742976 | bytes 88113152 | tf_op jit(solution)/shard_map/while/body/eval_jaxpr/dot_general | solution.py:40
  957.0 88.5 %fusion.183 = f32[4,512,3072]{2,1,0:T(8,128)} fusion(bf16[1,6144,3072]{2,1,0:T(8,128)(2,1)} %get-tuple-element.1044, bf16[4,512,6144]{2,1,0:T(8,128)(2,1)} %get-tuple-element.955, f32[6144]{0:T(1024)S(1)} %bitcast.168, f32[4,512]{1,0:T(4,128)S(1)} %add_rsqrt_fusion.13), kind=kOutput, calls=%fused_computation.25.clone.2 | convolution fusion | flops 77359742976 | bytes 88113152 | tf_op jit(solution)/shard_map/while/body/eval_jaxpr/dot_general | solution.py:40
  1045.6 96.9 %fusion.185 = bf16[4,512,6144]{2,1,0:T(8,128)(2,1)} fusion(bf16[1,3072,6144]{2,1,0:T(8,128)(2,1)} %get-tuple-element.1045, f32[4,512,3072]{2,1,0:T(8,128)} %fusion.183, f32[4,512,3072]{2,1,0:T(8,128)} %fusion.184), kind=kOutput, calls=%fused_computation.37.clone.2 | convolution fusion | flops 77359742976 | bytes 113246208 | tf_op jit(solution)/shard_map/while/body/eval_jaxpr/dot_general | solution.py:40
  1142.6 417.4 %all-reduce.8.cloned.1.call-done = bf16[4,512,6144]{2,1,0:T(8,128)(2,1)} async-done(((bf16[4,512,6144]{2,1,0:T(8,128)(2,1)}), bf16[4,512,6144]{2,1,0:T(8,128)(2,1)}) %all-reduce.8.cloned.1.call-update) | async-done | bytes 25165840 | tf_op jit(solution)/shard_map/while/body/eval_jaxpr/psum | solution.py:88
  1609.7 522.5 %collective-permute-done = bf16[4,512,6144]{2,1,0:T(8,128)(2,1)} collective-permute-done((bf16[4,512,6144]{2,1,0:T(8,128)(2,1)}, bf16[4,512,6144]{2,1,0:T(8,128)(2,1)}, u32[]{:S(2)}, u32[]{:S(2)}) %collective-permute-start) | collective-permute-done | bytes 25165856 | tf_op jit(solution)/shard_map/while/body/eval_jaxpr/ppermute | solution.py:131
  2468.5 60.6 fusion.181
  2529.9 416.5 %all-reduce.6.cloned.1.call-done = bf16[4,512,6144]{2,1,0:T(8,128)(2,1)} async-done(((bf16[4,512,6144]{2,1,0:T(8,128)(2,1)}), bf16[4,512,6144]{2,1,0:T(8,128)(2,1)}) %all-reduce.6.cloned.1.call-update) | async-done | bytes 25165840 | tf_op jit(solution)/shard_map/while/body/eval_jaxpr/psum | solution.py:84
  2976.9 88.3 %fusion.184 = f32[4,512,3072]{2,1,0:T(8,128)} fusion(bf16[1,6144,3072]{2,1,0:T(8,128)(2,1)} %get-tuple-element.1043, bf16[4,512,6144]{2,1,0:T(8,128)(2,1)} %get-tuple-element.955, f32[6144]{0:T(1024)S(1)} %bitcast.167, f32[4,512]{1,0:T(4,128)S(1)} %add_rsqrt_fusion.13), kind=kOutput, calls=%fused_computation.27.clone.1 | convolution fusion | flops 77359742976 | bytes 88113152 | tf_op jit(solution)/shard_map/while/body/eval_jaxpr/dot_general | solution.py:40
  3065.2 88.5 %fusion.183 = f32[4,512,3072]{2,1,0:T(8,128)} fusion(bf16[1,6144,3072]{2,1,0:T(8,128)(2,1)} %get-tuple-element.1044, bf16[4,512,6144]{2,1,0:T(8,128)(2,1)} %get-tuple-element.955, f32[6144]{0:T(1024)S(1)} %bitcast.168, f32[4,512]{1,0:T(4,128)S(1)} %add_rsqrt_fusion.13), kind=kOutput, calls=%fused_computation.25.clone.2 | convolution fusion | flops 77359742976 | bytes 88113152 | tf_op jit(solution)/shard_map/while/body/eval_jaxpr/dot_general | solution.py:40
  3153.7 96.9 %fusion.185 = bf16[4,512,6144]{2,1,0:T(8,128)(2,1)} fusion(bf16[1,3072,6144]{2,1,0:T(8,128)(2,1)} %get-tuple-element.1045, f32[4,512,3072]{2,1,0:T(8,128)} %fusion.183, f32[4,512,3072]{2,1,0:T(8,128)} %fusion.184), kind=kOutput, calls=%fused_computation.37.clone.2 | convolution fusion | flops 77359742976 | bytes 113246208 | tf_op jit(solution)/shard_map/while/body/eval_jaxpr/dot_general | solution.py:40
  3250.7 417.4 %all-reduce.8.cloned.1.call-done = bf16[4,512,6144]{2,1,0:T(8,128)(2,1)} async-done(((bf16[4,512,6144]{2,1,0:T(8,128)(2,1)}), bf16[4,512,6144]{2,1,0:T(8,128)(2,1)}) %all-reduce.8.cloned.1.call-update) | async-done | bytes 25165840 | tf_op jit(solution)/shard_map/while/body/eval_jaxpr/psum | solution.py:88
  3717.8 522.5 %collective-permute-done = bf16[4,512,6144]{2,1,0:T(8,128)(2,1)} collective-permute-done((bf16[4,512,6144]{2,1,0:T(8,128)(2,1)}, bf16[4,512,6144]{2,1,0:T(8,128)(2,1)}, u32[]{:S(2)}, u32[]{:S(2)}) %collective-permute-start) | collective-permute-done | bytes 25165856 | tf_op jit(solution)/shard_map/while/body/eval_jaxpr/ppermute | solution.py:131
  4323.5 60.2 all-gather.2.cloned.1.call-done
  4576.6 60.6 fusion.181
  4638.0 416.6 %all-reduce.6.cloned.1.call-done = bf16[4,512,6144]{2,1,0:T(8,128)(2,1)} async-done(((bf16[4,512,6144]{2,1,0:T(8,128)(2,1)}), bf16[4,512,6144]{2,1,0:T(8,128)(2,1)}) %all-reduce.6.cloned.1.call-update) | async-done | bytes 25165840 | tf_op jit(solution)/shard_map/while/body/eval_jaxpr/psum | solution.py:84
  5085.1 88.3 %fusion.184 = f32[4,512,3072]{2,1,0:T(8,128)} fusion(bf16[1,6144,3072]{2,1,0:T(8,128)(2,1)} %get-tuple-element.1043, bf16[4,512,6144]{2,1,0:T(8,128)(2,1)} %get-tuple-element.955, f32[6144]{0:T(1024)S(1)} %bitcast.167, f32[4,512]{1,0:T(4,128)S(1)} %add_rsqrt_fusion.13), kind=kOutput, calls=%fused_computation.27.clone.1 | convolution fusion | flops 77359742976 | bytes 88113152 | tf_op jit(solution)/shard_map/while/body/eval_jaxpr/dot_general | solution.py:40
  5173.3 88.5 %fusion.183 = f32[4,512,3072]{2,1,0:T(8,128)} fusion(bf16[1,6144,3072]{2,1,0:T(8,128)(2,1)} %get-tuple-element.1044, bf16[4,512,6144]{2,1,0:T(8,128)(2,1)} %get-tuple-element.955, f32[6144]{0:T(1024)S(1)} %bitcast.168, f32[4,512]{1,0:T(4,128)S(1)} %add_rsqrt_fusion.13), kind=kOutput, calls=%fused_computation.25.clone.2 | convolution fusion | flops 77359742976 | bytes 88113152 | tf_op jit(solution)/shard_map/while/body/eval_jaxpr/dot_general | solution.py:40
  5261.9 96.9 %fusion.185 = bf16[4,512,6144]{2,1,0:T(8,128)(2,1)} fusion(bf16[1,3072,6144]{2,1,0:T(8,128)(2,1)} %get-tuple-element.1045, f32[4,512,3072]{2,1,0:T(8,128)} %fusion.183, f32[4,512,3072]{2,1,0:T(8,128)} %fusion.184), kind=kOutput, calls=%fused_computation.37.clone.2 | convolution fusion | flops 77359742976 | bytes 113246208 | tf_op jit(solution)/shard_map/while/body/eval_jaxpr/dot_general | solution.py:40
  5358.9 417.4 %all-reduce.8.cloned.1.call-done = bf16[4,512,6144]{2,1,0:T(8,128)(2,1)} async-done(((bf16[4,512,6144]{2,1,0:T(8,128)(2,1)}), bf16[4,512,6144]{2,1,0:T(8,128)(2,1)}) %all-reduce.8.cloned.1.call-update) | async-done | bytes 25165840 | tf_op jit(solution)/shard_map/while/body/eval_jaxpr/psum | solution.py:88
  5826.0 522.5 %collective-permute-done = bf16[4,512,6144]{2,1,0:T(8,128)(2,1)} collective-permute-done((bf16[4,512,6144]{2,1,0:T(8,128)(2,1)}, bf16[4,512,6144]{2,1,0:T(8,128)(2,1)}, u32[]{:S(2)}, u32[]{:S(2)}) %collective-permute-start) | collective-permute-done | bytes 25165856 | tf_op jit(solution)/shard_map/while/body/eval_jaxpr/ppermute | solution.py:131
  (267 shorter events, 1165.6 us)
Async XLA Ops:
  23.0 144.2 %all-gather.2.cloned.1.call-start = ((), (), s32[]{:S(2)}) async-start(), calls=%async_computation.1 | async-start | bytes 11141120 | tf_op jit(solution)/shard_map/while/body/eval_jaxpr/all_gather | solution.py:75
  101.0 737.3 %all-reduce.6.cloned.1.call-start = ((), (), s32[]{:S(2)}) async-start(), calls=%async_computation.2 | async-start | bytes 50331648 | tf_op jit(solution)/shard_map/while/body/eval_jaxpr/psum | solution.py:84
  421.0 1139.0 %all-reduce.8.cloned.1.call-start = ((), (), s32[]{:S(2)}) async-start(), calls=%async_computation.3 | async-start | bytes 50331648 | tf_op jit(solution)/shard_map/while/body/eval_jaxpr/psum | solution.py:88
  1142.5 466.8 %copy-start.10 = (pred[4]{0:T(512)(128)(4,1)S(1)}, pred[4]{0:T(512)(128)(4,1)}, u32[]{:S(2)}) copy-start(pred[4]{0:T(512)(128)(4,1)} %get-tuple-element.957) | copy-start | bytes 16 | tf_op jit(solution)/shard_map/while
  1142.5 467.0 %copy-start.6 = (bf16[8,6144]{1,0:T(8,128)(2,1)S(1)}, bf16[8,6144]{1,0:T(8,128)(2,1)}, u32[]{:S(2)}) copy-start(bf16[8,6144]{1,0:T(8,128)(2,1)} %get-tuple-element.995) | copy-start | bytes 294916 | tf_op jit(solution)/shard_map/while
  1590.1 542.1 %collective-permute-start = (bf16[4,512,6144]{2,1,0:T(8,128)(2,1)}, bf16[4,512,6144]{2,1,0:T(8,128)(2,1)}, u32[]{:S(2)}, u32[]{:S(2)}) collective-permute-start(bf16[4,512,6144]{2,1,0:T(8,128)(2,1)} %fusion.186), channel_id=1, source_target_pairs={{0,4},{1,5},{2,6},{3,7}} | collective-permute-start | bytes 75497480 | tf_op jit(solution)/shard_map/while/body/eval_jaxpr/ppermute | solution.py:131
  1603.4 528.9 %copy-start.5 = (bf16[1,8,512,64]{2,3,1,0:T(8,128)(2,1)}, bf16[1,8,512,64]{2,3,1,0:T(8,128)(2,1)S(1)}, u32[]{:S(2)}) copy-start(bf16[1,8,512,64]{2,3,1,0:T(8,128)(2,1)S(1)} %constant_dynamic-update-slice_fusion.2) | copy-start | bytes 1572868 | tf_op jit(solution)/shard_map/while
  1609.7 522.5 %copy-start.7 = (bf16[8,6144]{1,0:T(8,128)(2,1)}, bf16[8,6144]{1,0:T(8,128)(2,1)S(1)}, u32[]{:S(2)}) copy-start(bf16[8,6144]{1,0:T(8,128)(2,1)S(1)} %fusion.189) | copy-start | bytes 294916 | tf_op jit(solution)/shard_map/while
  2132.4 143.2 %all-gather.2.cloned.1.call-start = ((), (), s32[]{:S(2)}) async-start(), calls=%async_computation.1 | async-start | bytes 11141120 | tf_op jit(solution)/shard_map/while/body/eval_jaxpr/all_gather | solution.py:75
  2210.5 736.0 %all-reduce.6.cloned.1.call-start = ((), (), s32[]{:S(2)}) async-start(), calls=%async_computation.2 | async-start | bytes 50331648 | tf_op jit(solution)/shard_map/while/body/eval_jaxpr/psum | solution.py:84
  2529.1 1139.0 %all-reduce.8.cloned.1.call-start = ((), (), s32[]{:S(2)}) async-start(), calls=%async_computation.3 | async-start | bytes 50331648 | tf_op jit(solution)/shard_map/while/body/eval_jaxpr/psum | solution.py:88
  3250.7 466.7 %copy-start.10 = (pred[4]{0:T(512)(128)(4,1)S(1)}, pred[4]{0:T(512)(128)(4,1)}, u32[]{:S(2)}) copy-start(pred[4]{0:T(512)(128)(4,1)} %get-tuple-element.957) | copy-start | bytes 16 | tf_op jit(solution)/shard_map/while
  3250.7 467.0 %copy-start.6 = (bf16[8,6144]{1,0:T(8,128)(2,1)S(1)}, bf16[8,6144]{1,0:T(8,128)(2,1)}, u32[]{:S(2)}) copy-start(bf16[8,6144]{1,0:T(8,128)(2,1)} %get-tuple-element.995) | copy-start | bytes 294916 | tf_op jit(solution)/shard_map/while
  3698.3 542.1 %collective-permute-start = (bf16[4,512,6144]{2,1,0:T(8,128)(2,1)}, bf16[4,512,6144]{2,1,0:T(8,128)(2,1)}, u32[]{:S(2)}, u32[]{:S(2)}) collective-permute-start(bf16[4,512,6144]{2,1,0:T(8,128)(2,1)} %fusion.186), channel_id=1, source_target_pairs={{0,4},{1,5},{2,6},{3,7}} | collective-permute-start | bytes 75497480 | tf_op jit(solution)/shard_map/while/body/eval_jaxpr/ppermute | solution.py:131
  3711.5 528.9 %copy-start.5 = (bf16[1,8,512,64]{2,3,1,0:T(8,128)(2,1)}, bf16[1,8,512,64]{2,3,1,0:T(8,128)(2,1)S(1)}, u32[]{:S(2)}) copy-start(bf16[1,8,512,64]{2,3,1,0:T(8,128)(2,1)S(1)} %constant_dynamic-update-slice_fusion.2) | copy-start | bytes 1572868 | tf_op jit(solution)/shard_map/while
  3717.8 522.5 %copy-start.7 = (bf16[8,6144]{1,0:T(8,128)(2,1)}, bf16[8,6144]{1,0:T(8,128)(2,1)S(1)}, u32[]{:S(2)}) copy-start(bf16[8,6144]{1,0:T(8,128)(2,1)S(1)} %fusion.189) | copy-start | bytes 294916 | tf_op jit(solution)/shard_map/while
  4240.5 143.2 %all-gather.2.cloned.1.call-start = ((), (), s32[]{:S(2)}) async-start(), calls=%async_computation.1 | async-start | bytes 11141120 | tf_op jit(solution)/shard_map/while/body/eval_jaxpr/all_gather | solution.py:75
  4318.6 736.0 %all-reduce.6.cloned.1.call-start = ((), (), s32[]{:S(2)}) async-start(), calls=%async_computation.2 | async-start | bytes 50331648 | tf_op jit(solution)/shard_map/while/body/eval_jaxpr/psum | solution.py:84
  4637.3 1139.1 %all-reduce.8.cloned.1.call-start = ((), (), s32[]{:S(2)}) async-start(), calls=%async_computation.3 | async-start | bytes 50331648 | tf_op jit(solution)/shard_map/while/body/eval_jaxpr/psum | solution.py:88
  5358.9 467.0 %copy-start.6 = (bf16[8,6144]{1,0:T(8,128)(2,1)S(1)}, bf16[8,6144]{1,0:T(8,128)(2,1)}, u32[]{:S(2)}) copy-start(bf16[8,6144]{1,0:T(8,128)(2,1)} %get-tuple-element.995) | copy-start | bytes 294916 | tf_op jit(solution)/shard_map/while
  5806.4 542.1 %collective-permute-start = (bf16[4,512,6144]{2,1,0:T(8,128)(2,1)}, bf16[4,512,6144]{2,1,0:T(8,128)(2,1)}, u32[]{:S(2)}, u32[]{:S(2)}) collective-permute-start(bf16[4,512,6144]{2,1,0:T(8,128)(2,1)} %fusion.186), channel_id=1, source_target_pairs={{0,4},{1,5},{2,6},{3,7}} | collective-permute-start | bytes 75497480 | tf_op jit(solution)/shard_map/while/body/eval_jaxpr/ppermute | solution.py:131
  5819.7 528.9 %copy-start.5 = (bf16[1,8,512,64]{2,3,1,0:T(8,128)(2,1)}, bf16[1,8,512,64]{2,3,1,0:T(8,128)(2,1)S(1)}, u32[]{:S(2)}) copy-start(bf16[1,8,512,64]{2,3,1,0:T(8,128)(2,1)S(1)} %constant_dynamic-update-slice_fusion.2) | copy-start | bytes 1572868 | tf_op jit(solution)/shard_map/while
  5826.0 522.5 %copy-start.7 = (bf16[8,6144]{1,0:T(8,128)(2,1)}, bf16[8,6144]{1,0:T(8,128)(2,1)S(1)}, u32[]{:S(2)}) copy-start(bf16[8,6144]{1,0:T(8,128)(2,1)S(1)} %fusion.189) | copy-start | bytes 294916 | tf_op jit(solution)/shard_map/while
  6349.6 20.5 all-reduce.4.cloned.1.call-start
  (25 other events, 6151.7 us)
Sparse Core Ops, SparseCore 0:
  101.1 66.0 all-gather.1
  421.1 417.1 all-reduce.5
  1142.6 417.3 all-reduce.7
  2210.6 64.9 all-gather.1
  2529.3 417.1 all-reduce.5
  3250.8 417.3 all-reduce.7
  4318.7 64.9 all-gather.1
  4637.4 417.1 all-reduce.5
  5358.9 417.3 all-reduce.7
Sparse Core Ops, SparseCore 1:
  6352.9 17.1 all-reduce.3
where the time goes:
time: 6380 us
  waiting for transfers between devices  4270 us (67%)
  matrix products  1520 us (24%)
  other arithmetic  396 us (6%)
  local copies, waits for them, and re-layouts  133 us (2%)
    ppermute x3, waiting for transfers between devices, tick_step(): inbox = lax.ppermute(hidden, 'pp', shift_pairs)  1570 us
    psum x3, waiting for transfers between devices, layer_step(): hidden = residual(hidden, lax.psum(mlp_part, 'tp'), res_scale)  1250 us
    psum x3, waiting for transfers between devices, layer_step(): hidden = residual(hidden, lax.psum(attn_part, 'tp'), res_scale)  1250 us
    dot_general x24, matrix products, matmul_f32(): return jnp.dot(act_in, weight, preferred_element_type=jnp.float32)  1190 us
    all_gather x3, waiting for transfers between devices, layer_step(): lax.all_gather(joined, 'tp', axis=0, tiled=True)  181 us
    reduce_sum x12, other arithmetic, rms_norm(): jnp.mean(wide_vals * wide_vals, axis=-1, keepdims=True) + RMS_EPS  169 us
    sub x3, matrix products, attend(): jax.nn.softmax(jnp.where(allowed, scores, -1e+30), axis=-1)  164 us
  transfers between devices with their start and end apart: 13, of which 13 were waited for; matrix products, arithmetic and copies ran while one was open for 1% of the time, Pallas kernels for 0%

commit v1 on v0

v1 whole, which is shorter than its diff:
```python
import functools
import math
import jax
import jax.numpy as jnp
from jax import lax
from jax.experimental import pallas as pl
from jax.experimental.pallas import tpu as pltpu
from jax.sharding import Mesh, PartitionSpec as P

RMS_EPS = 1e-5
ROPE_BASE = 10000.0
SCALE_DEPTH = 1.4
BF16, F32 = jnp.bfloat16, jnp.float32
ROWS = 128
HEAD_BLOCK = 4
OUT_COLS = 768
ACT_COLS = 256
DOWN_COLS = 256
VMEM_LIMIT = 60 * 2 ** 20


def dot(lhs, rhs):
    return jnp.dot(lhs, rhs, preferred_element_type=F32)


def dot_t(lhs, rhs):
    return lax.dot_general(lhs, rhs, (((1,), (1,)), ((), ())), preferred_element_type=F32)


def rms_wide(wide, gain):
    inv = lax.rsqrt(jnp.mean(wide * wide, axis=-1, keepdims=True) + RMS_EPS)
    return (wide * inv * gain).astype(BF16)


def rms_rows(x_ref, rows, count, gain_ref, out_ref):
    width, cols = x_ref.shape[1], 256
    squares = jnp.zeros((count, cols), F32)
    for first in range(0, width, cols):
        wide = x_ref[rows, first:first + cols].astype(F32)
        squares = squares + wide * wide
    inv = lax.rsqrt(jnp.sum(squares, axis=-1, keepdims=True) * (1.0 / width) + RMS_EPS)
    for first in range(0, width, cols):
        wide = x_ref[rows, first:first + cols].astype(F32)
        out_ref[rows, first:first + cols] = (wide * inv * gain_ref[:, first:first + cols].astype(F32)).astype(BF16)


def rms_norm(values_in, gain):
    return rms_wide(values_in.astype(F32), gain.astype(F32))


def rope_tables(seq, rope):
    inv_freq = ROPE_BASE ** (-2.0 * jnp.arange(rope // 2, dtype=F32) / rope)
    angle = jnp.arange(seq, dtype=F32)[:, None] * inv_freq[None, :]
    cos_t, sin_t = jnp.cos(angle), jnp.sin(angle)
    return jnp.concatenate([cos_t, cos_t], axis=-1), jnp.concatenate([-sin_t, sin_t], axis=-1)


def apply_rope(values_in, cos_t, sin_t):
    half = values_in.shape[-1] // 2
    wide = values_in.astype(F32)
    swapped = jnp.concatenate([wide[..., half:], wide[..., :half]], axis=-1)
    return (wide * cos_t + swapped * sin_t).astype(BF16)


def call(kernel, grid, scalars, inputs, outputs, scratch, flops, moved):
    return pl.pallas_call(
        kernel,
        grid_spec=pltpu.PrefetchScalarGridSpec(
            num_scalar_prefetch=1, grid=grid,
            in_specs=[spec for _, spec in inputs], out_specs=[spec for _, spec in outputs], scratch_shapes=scratch),
        out_shape=[jax.ShapeDtypeStruct(shape, dtype) for (shape, dtype), _ in outputs],
        compiler_params=pltpu.CompilerParams(dimension_semantics=("arbitrary",) * len(grid), vmem_limit_bytes=VMEM_LIMIT),
        cost_estimate=pl.CostEstimate(flops=int(flops), transcendentals=0, bytes_accessed=int(moved)),
    )(scalars, *[array for array, _ in inputs])


ANY = pl.BlockSpec(memory_space=pl.ANY)
TOKEN = ((8, 128), F32)


def fixed(*shape):
    return pl.BlockSpec(shape, lambda *_: (0,) * len(shape))


ORDER = [
    ("down", 0), ("att", 0), ("down", 1), ("suma", 0), ("att", 1), ("down", 2),
    ("suma", 1), ("res", 0), ("att", 2), ("down", 3), ("res", 1), ("att", 3),
    ("suma", 2), ("mlp", 0), ("res", 2), ("suma", 3), ("mlp", 1), ("summ", 0),
    ("res", 3), ("summ", 1), ("mlp", 2), ("next", 0), ("summ", 2), ("mlp", 3),
    ("next", 1), ("summ", 3), ("next", 2), ("next", 3),
]


def down_kernel(dims, info, x_ref, g_attn, wq_ref, g_q, wkv_hbm, g_kv, cos_ref, sin_ref, _, joined_ref, token_ref,
                u_ref, raw_ref, wkv_ref, sem):
    q_rank, kv_rank, rope, steps = dims
    step = pl.program_id(0)
    active = info[0] == 1
    copy = pltpu.make_async_copy(wkv_hbm, wkv_ref, sem)
    seq = x_ref.shape[0]

    @pl.when((step == 0) & active)
    def _():
        copy.start()
        for first in range(0, seq, ROWS):
            for inner in range(first, first + ROWS, 32):
                rms_rows(x_ref, pl.ds(inner, 32), 32, g_attn, u_ref)
            rows = pl.ds(first, ROWS)
            raw_ref[rows, :DOWN_COLS] = dot(u_ref[rows, :], wq_ref[...]).astype(BF16)

    @pl.when((step > 0) & (step < steps) & active)
    def _():
        cols = pl.ds(pl.multiple_of(step * DOWN_COLS, DOWN_COLS), DOWN_COLS)
        raw_ref[:, cols] = dot(u_ref[...], wq_ref[...]).astype(BF16)

    @pl.when((step == steps) & active)
    def _():
        copy.wait()
        low = dot_t(u_ref[...], wkv_ref[...]).astype(BF16)
        for first in range(0, seq, 32):
            rows = pl.ds(first, 32)
            joined_ref[rows, :q_rank] = rms_norm(raw_ref[rows, :], g_q[...])
            joined_ref[rows, q_rank:q_rank + kv_rank] = rms_norm(low[first:first + 32, :kv_rank], g_kv[...])
            joined_ref[rows, q_rank + kv_rank:] = jnp.concatenate(
                [apply_rope(low[first:first + 32, kv_rank:], cos_ref[rows, :], sin_ref[rows, :]), jnp.zeros((32, rope), BF16)], axis=-1)

    @pl.when(step == steps)
    def _():
        token_ref[...] = jnp.zeros_like(token_ref)


def attention_kernel(dims, info, own_hbm, other_hbm, wq_ref, wkv_ref, wo_ref, cos_ref, sin_ref, _, near_ref, far_ref, token_ref,
                     joined, outs, sems):
    q_rank, kv_rank, nope, rope, v_head, steps = dims
    step = pl.program_id(0)
    active = info[0] == 1
    qk, seq = nope + rope, joined.shape[1]
    copies = [pltpu.make_async_copy(ref, joined.at[i], sems.at[i]) for i, ref in enumerate((own_hbm, other_hbm))]

    @pl.when((step == 0) & active)
    def _():
        copies[0].start()
        copies[1].start()
        copies[0].wait()

    @pl.when((step == 1) & active)
    def _():
        copies[1].wait()

    @pl.when((step < steps) & active)
    def _():
        prompt = step % 2
        length = info[2 + prompt]
        chip = info[1]
        q_all = dot(joined[prompt, :, :q_rank], wq_ref[...]).astype(BF16)
        kv_all = dot(joined[prompt, :, q_rank:q_rank + kv_rank], wkv_ref[...]).astype(BF16)
        k_rope = joined[prompt, :, q_rank + kv_rank:q_rank + kv_rank + rope]
        cos_t, sin_t = cos_ref[...], sin_ref[...]
        for head in range(HEAD_BLOCK):
            q_rope = apply_rope(q_all[:, head * qk + nope:(head + 1) * qk], cos_t, sin_t)
            queries = jnp.concatenate([q_all[:, head * qk:head * qk + nope], q_rope], axis=-1)
            base = head * (nope + v_head)
            keys = jnp.concatenate([kv_all[:, base:base + nope], k_rope], axis=-1)
            values = kv_all[:, base + nope:base + nope + v_head]
            cols = pl.ds(pl.multiple_of(((step // 2) * HEAD_BLOCK + head) * v_head, v_head), v_head)
            for first in range(0, seq, ROWS):
                ends = first + ROWS
                scores = lax.dot_general(queries[first:ends], keys[:ends], (((1,), (1,)), ((), ())),
                                         preferred_element_type=F32) * (qk ** -0.5 * math.log2(math.e))
                limit = jnp.minimum(lax.broadcasted_iota(jnp.int32, (ROWS, 1), 0) + first, length - 1)
                scores = jnp.where(lax.broadcasted_iota(jnp.int32, (ROWS, ends), 1) <= limit, scores, -1e30)
                grown = jnp.exp2(scores - jnp.max(scores, axis=-1, keepdims=True))
                probs = (grown * (1.0 / jnp.sum(grown, axis=-1, keepdims=True))).astype(BF16)
                half = seq // 2
                place = jnp.bitwise_xor(first // half, chip) * half + first % half
                outs[prompt, pl.ds(pl.multiple_of(place, ROWS), ROWS), cols] = dot(probs, values[:ends]).astype(BF16)

    @pl.when((step >= steps) & active)
    def _():
        for prompt, out_ref in enumerate((near_ref, far_ref)):
            for first in range(0, seq, 256):
                out_ref[pl.ds(first, 256), :] = dot(outs[prompt, pl.ds(first, 256), :], wo_ref[...]).astype(BF16)

    @pl.when(step == pl.num_programs(0) - 1)
    def _():
        token_ref[...] = jnp.zeros_like(token_ref)


def mlp_kernel(steps, info, m0, m1, m2, m3, w1_ref, w3_ref, w2_ref, _, near_ref, far_ref, token_ref, rows_ref, act_ref, sems):
    step = pl.program_id(0)
    active = info[0] == 1
    piece = m0.shape[0]
    copies = [pltpu.make_async_copy(ref, rows_ref.at[pl.ds(i * piece, piece)], sems.at[i]) for i, ref in enumerate((m0, m1, m2, m3))]

    def gate(first_step):
        cols = pl.ds(pl.multiple_of(step * ACT_COLS, ACT_COLS), ACT_COLS)
        for i in range(4):
            if first_step:
                copies[i].wait()
            rows = pl.ds(i * piece, piece)
            wide = dot(rows_ref[rows, :], w1_ref[...])
            act_ref[rows, cols] = (wide * jax.nn.sigmoid(wide) * dot(rows_ref[rows, :], w3_ref[...])).astype(BF16)

    @pl.when((step == 0) & active)
    def _():
        for copy in copies:
            copy.start()
        gate(True)

    @pl.when((step > 0) & (step < steps) & active)
    def _():
        gate(False)

    @pl.when((step >= steps) & active)
    def _():
        for i in range(4):
            out_ref = near_ref if i < 2 else far_ref
            out_ref[pl.ds((i % 2) * piece, piece), :] = dot(act_ref[pl.ds(i * piece, piece), :], w2_ref[...]).astype(BF16)

    @pl.when(step == pl.num_programs(0) - 1)
    def _():
        token_ref[...] = jnp.zeros_like(token_ref)


def add_kernel(info, a_ref, b_ref, _, out_ref, token_ref):
    out_ref[...] = (a_ref[...].astype(F32) + b_ref[...].astype(F32)).astype(BF16)
    token_ref[...] = jnp.zeros_like(token_ref)


def join(scale, hidden, near, other_core, other_chip):
    both = (near.astype(F32) + other_core.astype(F32)).astype(BF16)
    branch = (both.astype(F32) + other_chip.astype(F32)).astype(BF16)
    return (hidden.astype(F32) + scale * branch.astype(F32)).astype(BF16)


def residual_kernel(scale, info, x_ref, near_ref, core_ref, chip_ref, gain, _, h_ref, m_ref, token_ref):
    hidden = join(scale, x_ref[...], near_ref[...], core_ref[...], chip_ref[...])
    h_ref[...] = hidden
    m_ref[...] = rms_norm(hidden, gain[...])
    token_ref[...] = jnp.zeros_like(token_ref)


def next_kernel(scale, kv_rank, info, h_ref, near_ref, core_ref, chip_ref, g_attn, wkv_ref, g_kv, cos_ref, sin_ref, _,
                msg_ref, token_ref, row_ref):
    step = pl.program_id(0)
    rows = h_ref.shape[0]
    total = rows * pl.num_programs(0)
    hidden = join(scale, h_ref[...], near_ref[...], core_ref[...], chip_ref[...])
    low = dot_t(rms_norm(hidden, g_attn[...]), wkv_ref[...]).astype(BF16)
    msg_ref[pl.ds(pl.multiple_of(step * rows, rows), rows), :kv_rank] = rms_norm(low[:, :kv_rank], g_kv[...])
    turned = apply_rope(low[:, kv_rank:], cos_ref[...], sin_ref[...])
    msg_ref[pl.ds(pl.multiple_of(step * rows, rows), rows), kv_rank:] = jnp.concatenate([turned, jnp.zeros_like(turned)], axis=-1)
    wanted = info[2] - 1 - info[1] * total - step * rows
    picked = jnp.where(lax.broadcasted_iota(jnp.int32, (rows, 1), 0) == wanted, hidden.astype(F32), 0.0)
    picked = jnp.sum(picked, axis=0, keepdims=True)

    @pl.when(step == 0)
    def _():
        row_ref[...] = jnp.broadcast_to(picked, row_ref.shape)

    @pl.when(step > 0)
    def _():
        row_ref[...] += jnp.broadcast_to(picked, row_ref.shape)

    @pl.when(step == pl.num_programs(0) - 1)
    def _():
        width = msg_ref.shape[1]
        depth = row_ref.shape[1]
        parts = []
        for first in range(0, depth, width):
            part = row_ref[0:1, first:min(first + width, depth)]
            if part.shape[1] < width:
                part = jnp.concatenate([part, jnp.zeros((1, width - part.shape[1]), F32)], axis=-1)
            parts.append(part)
        parts.append(jnp.zeros((16 - len(parts), width), F32))
        msg_ref[pl.ds(total, 16), :] = jnp.concatenate(parts, axis=0).astype(BF16)

    token_ref[...] = jnp.zeros_like(token_ref)


def last_kernel(dims, info, q_ref, c_ref, wkv_ref, out_ref):
    kv_rank, nope, rope, v_head = dims
    for prompt in range(2):
        length = info[2 + prompt]
        kv_all = dot(c_ref[prompt, :, :kv_rank], wkv_ref[...]).astype(BF16)
        k_rope = c_ref[prompt, :, kv_rank:kv_rank + rope]
        for head in range(HEAD_BLOCK):
            base = head * (nope + v_head)
            keys = jnp.concatenate([kv_all[:, base:base + nope], k_rope], axis=-1)
            query = q_ref[prompt, head]
            scores = lax.dot_general(query, keys, (((1,), (1,)), ((), ())), preferred_element_type=F32) * (nope + rope) ** -0.5
            scores = jnp.where(lax.broadcasted_iota(jnp.int32, scores.shape, 1) < length, scores, -1e30)
            grown = jnp.exp(scores - jnp.max(scores, axis=-1, keepdims=True))
            probs = (grown * (1.0 / jnp.sum(grown, axis=-1, keepdims=True))).astype(BF16)
            out_ref[prompt, :, head * v_head:(head + 1) * v_head] = dot(probs, kv_all[:, base + nope:base + nope + v_head]).astype(BF16)


def rows_kernel(info, rows_ref, w_ref, out_ref):
    out_ref[...] = dot(rows_ref[...], w_ref[...]).astype(BF16)


def rows_mlp_kernel(steps, info, rows_ref, w1_ref, w3_ref, w2_ref, out_ref, act_ref):
    step = pl.program_id(0)

    @pl.when(step < steps)
    def _():
        wide = dot(rows_ref[...], w1_ref[...])
        cols = pl.ds(pl.multiple_of(step * ACT_COLS, ACT_COLS), ACT_COLS)
        act_ref[:, cols] = (wide * jax.nn.sigmoid(wide) * dot(rows_ref[...], w3_ref[...])).astype(BF16)

    @pl.when(step >= steps)
    def _():
        out_ref[...] = dot(act_ref[...], w2_ref[...]).astype(BF16)


def solution(mesh):
    dp_size, pp_size, tp_size = mesh.shape["dp"], mesh.shape["pp"], mesh.shape["tp"]
    grid = Mesh(mesh.devices.reshape(dp_size, pp_size, tp_size // 2, 2), ("dp", "pp", "x", "core"))
    down, up = [(0, 1)], [(1, 0)]

    def program(x_in, seq_len, norm_attn, w_qa, norm_q, w_qb, w_kva, norm_kv, w_kvb, w_o, norm_mlp, w_gate, w_up, w_down, norm_final):
        batch, seq, width = x_in.shape
        wq_down, wq_up, wkv_down, wkv_up = w_qa[0], w_qb[0], w_kva[0].T, w_kvb[0]
        wo_part, w1_part, w3_part, w2_part = w_o[0], w_gate[0], w_up[0], w_down[0]
        q_rank, kv_rank = norm_q.shape[1], norm_kv.shape[1]
        rope = wkv_down.shape[0] - kv_rank
        heads = (wq_up.shape[1] - wkv_up.shape[1] + wo_part.shape[0]) // rope
        v_head = wo_part.shape[0] // heads
        nope = wkv_up.shape[1] // heads - v_head
        hidden_cols = w1_part.shape[1]
        scale = SCALE_DEPTH / math.sqrt(w_qa.shape[0] * pp_size)
        stage, chip, core = (lax.axis_index(name).astype(jnp.int32) for name in ("pp", "x", "core"))
        active = (stage == 0).astype(jnp.int32)
        cos_t, sin_t = rope_tables(seq, rope)
        flat_x = x_in.reshape(batch * seq, width)
        half = seq // 2
        joined_cols = q_rank + kv_rank + 2 * rope
        msg_cols = kv_rank + 2 * rope
        chunks = batch // 2

        next_wkv = lax.ppermute(wkv_down, "pp", up)
        next_g_attn = lax.ppermute(norm_attn, "pp", up)
        next_g_kv = lax.ppermute(norm_kv, "pp", up)

        def down_proj(i, token):
            info = jnp.stack([active, 2 * i + core])
            steps = q_rank // DOWN_COLS
            return call(
                functools.partial(down_kernel, (q_rank, kv_rank, rope, steps)), (steps + 1,), info,
                [(flat_x, pl.BlockSpec((seq, width), lambda n, s: (s[1], 0))), (norm_attn, fixed(1, width)),
                 (wq_down, pl.BlockSpec((width, DOWN_COLS), lambda n, s: (0, jnp.minimum(n, steps - 1)))), (norm_q, fixed(1, q_rank)),
                 (wkv_down, ANY), (norm_kv, fixed(1, kv_rank)), (cos_t, fixed(seq, rope)), (sin_t, fixed(seq, rope)), (token, ANY)],
                [(((seq, joined_cols), BF16), fixed(seq, joined_cols)), (TOKEN, fixed(8, 128))],
                [pltpu.VMEM((seq, width), BF16), pltpu.VMEM((seq, q_rank), BF16), pltpu.VMEM(wkv_down.shape, BF16), pltpu.SemaphoreType.DMA],
                2 * seq * width * (q_rank + kv_rank + rope), 2 * (seq * width + width * joined_cols))

        def attention(i, own, other, token):
            lens = lax.slice_in_dim(seq_len, 2 * i, 2 * i + 2)
            info = jnp.stack([active, chip, jnp.where(core == 0, lens[0], lens[1]), jnp.where(core == 0, lens[1], lens[0])])
            steps, q_cols, kv_cols = 2 * heads // HEAD_BLOCK, HEAD_BLOCK * (nope + rope), HEAD_BLOCK * (nope + v_head)
            first = lambda n: jnp.minimum(n, steps - 1) // 2
            later = lambda n: jnp.maximum(n - steps, 0)
            out = (((seq, width), BF16), pl.BlockSpec((seq, OUT_COLS), lambda n, s: (0, later(n))))
            return call(
                functools.partial(attention_kernel, (q_rank, kv_rank, nope, rope, v_head, steps)), (steps + width // OUT_COLS,), info,
                [(own, ANY), (other, ANY), (wq_up, pl.BlockSpec((q_rank, q_cols), lambda n, s: (0, first(n)))),
                 (wkv_up, pl.BlockSpec((kv_rank, kv_cols), lambda n, s: (0, first(n)))),
                 (wo_part, pl.BlockSpec((heads * v_head, OUT_COLS), lambda n, s: (0, later(n)))),
                 (cos_t, fixed(seq, rope)), (sin_t, fixed(seq, rope)), (token, ANY)],
                [out, out, (TOKEN, fixed(8, 128))],
                [pltpu.VMEM((2, seq, joined_cols), BF16), pltpu.VMEM((2, seq, heads * v_head), BF16), pltpu.SemaphoreType.DMA((2,))],
                2 * 2 * seq * (q_rank * wq_up.shape[1] + kv_rank * wkv_up.shape[1] + heads * v_head * width + heads * 3 * v_head * seq),
                2 * (wq_up.size + wkv_up.size + wo_part.size + 2 * seq * width))

        def mlp(pieces, token):
            steps = hidden_cols // ACT_COLS
            first = lambda n: jnp.minimum(n, steps - 1)
            later = lambda n: jnp.maximum(n - steps, 0)
            out = (((seq, width), BF16), pl.BlockSpec((seq, OUT_COLS), lambda n, s: (0, later(n))))
            return call(
                functools.partial(mlp_kernel, steps), (steps + width // OUT_COLS,), jnp.stack([active, active]),
                [(m, ANY) for m in pieces] + [
                    (w1_part, pl.BlockSpec((width, ACT_COLS), lambda n, s: (0, first(n)))),
                    (w3_part, pl.BlockSpec((width, ACT_COLS), lambda n, s: (0, first(n)))),
                    (w2_part, pl.BlockSpec((hidden_cols, OUT_COLS), lambda n, s: (0, later(n)))), (token, ANY)],
                [out, out, (TOKEN, fixed(8, 128))],
                [pltpu.VMEM((2 * seq, width), BF16), pltpu.VMEM((2 * seq, hidden_cols), BF16), pltpu.SemaphoreType.DMA((4,))],
                2 * 2 * seq * width * hidden_cols * 3, 2 * (3 * width * hidden_cols + 4 * seq * width))

        ROW_STEP = 64
        low_rows = pl.BlockSpec((ROW_STEP, width), lambda n, s: (n, 0))
        high_rows = pl.BlockSpec((ROW_STEP, width), lambda n, s: (half // ROW_STEP + n, 0))

        def half_sum(near, other, token):
            return call(add_kernel, (half // ROW_STEP,), jnp.stack([active]),
                        [(near, high_rows), (other, high_rows), (token, ANY)],
                        [(((half, width), BF16), low_rows), (TOKEN, fixed(8, 128))], [], half * width, 6 * half * width)

        def residual(i, near, other, from_chip, token):
            info = jnp.stack([((2 * i + core) * 2 + chip) * (half // ROW_STEP)])
            return call(functools.partial(residual_kernel, scale), (half // ROW_STEP,), info,
                        [(flat_x, pl.BlockSpec((ROW_STEP, width), lambda n, s: (s[0] + n, 0))), (near, low_rows), (other, low_rows),
                         (from_chip, low_rows), (norm_mlp, fixed(1, width)), (token, ANY)],
                        [(((half, width), BF16), low_rows), (((half, width), BF16), low_rows), (TOKEN, fixed(8, 128))],
                        [], 8 * half * width, 12 * half * width)

        def next_latent(i, hidden, near, other, from_chip, token):
            mine = lax.slice_in_dim(seq_len, 2 * i, 2 * i + 2)
            info = jnp.stack([chip * (half // ROWS), chip, jnp.where(core == 0, mine[0], mine[1])])
            table = pl.BlockSpec((ROWS, rope), lambda n, s: (s[0] + n, 0))
            low = pl.BlockSpec((ROWS, width), lambda n, s: (n, 0))
            return call(functools.partial(next_kernel, scale, kv_rank), (half // ROWS,), info,
                        [(hidden, low), (near, low), (other, low), (from_chip, low), (next_g_attn, fixed(1, width)),
                         (next_wkv, fixed(*next_wkv.shape)), (next_g_kv, fixed(1, kv_rank)), (cos_t, table), (sin_t, table), (token, ANY)],
                        [(((half + 16, msg_cols), BF16), fixed(half + 16, msg_cols)), (TOKEN, fixed(8, 128))],
                        [pltpu.VMEM((8, width), F32)], 2 * half * width * (kv_rank + rope), 8 * half * width + 2 * next_wkv.size)

        def last_attention(lens, latent, rows):
            normed = rms_norm(rows, norm_attn[0])
            q_full = dot(rms_norm(dot(normed, wq_down).astype(BF16), norm_q[0]), wq_up).astype(BF16).reshape(2, heads, nope + rope)
            at = lens - 1
            q_full = jnp.concatenate([q_full[..., :nope], apply_rope(q_full[..., nope:], cos_t[at][:, None], sin_t[at][:, None])], axis=-1)
            q_full = jnp.broadcast_to(q_full[:, :, None], (2, heads, 16, nope + rope))
            info = jnp.concatenate([jnp.zeros((2,), jnp.int32), lens])
            blocks = heads // HEAD_BLOCK
            outs = call(functools.partial(last_kernel, (kv_rank, nope, rope, v_head)), (blocks,), info,
                        [(q_full, pl.BlockSpec((2, HEAD_BLOCK, 16, nope + rope), lambda n, s: (0, n, 0, 0))), (latent, fixed(2, seq, msg_cols)),
                         (wkv_up, pl.BlockSpec((kv_rank, HEAD_BLOCK * (nope + v_head)), lambda n, s: (0, n)))],
                        [(((2, 16, heads * v_head), BF16), pl.BlockSpec((2, 16, HEAD_BLOCK * v_head), lambda n, s: (0, 0, n)))],
                        [], 4 * seq * kv_rank * wkv_up.shape[1], 2 * wkv_up.size)[0]
            return outs[:, 0]

        def rows_matmul(rows, weight):
            count, depth = rows.shape
            return call(rows_kernel, (width // OUT_COLS,), jnp.stack([active]),
                        [(rows, fixed(count, depth)), (weight, pl.BlockSpec((depth, OUT_COLS), lambda n, s: (0, n)))],
                        [(((count, width), BF16), pl.BlockSpec((count, OUT_COLS), lambda n, s: (0, n)))],
                        [], 2 * count * weight.size, 2 * weight.size)[0]

        def rows_mlp(rows):
            count = rows.shape[0]
            steps = hidden_cols // ACT_COLS
            first = lambda n: jnp.minimum(n, steps - 1)
            later = lambda n: jnp.maximum(n - steps, 0)
            return call(functools.partial(rows_mlp_kernel, steps), (steps + width // OUT_COLS,), jnp.stack([active]),
                        [(rows, fixed(count, width)), (w1_part, pl.BlockSpec((width, ACT_COLS), lambda n, s: (0, first(n)))),
                         (w3_part, pl.BlockSpec((width, ACT_COLS), lambda n, s: (0, first(n)))),
                         (w2_part, pl.BlockSpec((hidden_cols, OUT_COLS), lambda n, s: (0, later(n))))],
                        [(((count, width), BF16), pl.BlockSpec((count, OUT_COLS), lambda n, s: (0, later(n))))],
                        [pltpu.VMEM((count, hidden_cols), BF16)], 6 * count * w1_part.size, 6 * w1_part.size)[0]

        token = jnp.zeros(*TOKEN)
        state = [dict() for _ in range(chunks)]

        def swap(value, axis, stage_of):
            return lax.ppermute(value, ("pp", axis), [(2 * stage_of, 2 * stage_of + 1), (2 * stage_of + 1, 2 * stage_of)])

        def run_down(i):
            nonlocal token
            own, token = down_proj(i, token)
            state[i].update(own=own, other=swap(own, "core", 0))

        def run_att(i):
            nonlocal token
            near, far, token = attention(i, state[i]["own"], state[i]["other"], token)
            state[i].update(near=near, from_core=swap(far, "core", 0))

        def run_suma(i):
            nonlocal token
            sent, token = half_sum(state[i]["near"], state[i]["from_core"], token)
            state[i].update(from_chip=swap(sent, "x", 0))

        run_summ = run_suma

        def run_res(i):
            nonlocal token
            s = state[i]
            s["hidden"], normed, token = residual(i, s["near"], s["from_core"], s["from_chip"], token)
            over = swap(normed, "x", 0)
            beside = swap(normed, "core", 0)
            s["pieces"] = (normed, over, beside, swap(over, "core", 0))

        def run_mlp(i):
            nonlocal token
            near, far, token = mlp(state[i]["pieces"], token)
            state[i].update(near=near, from_core=swap(far, "core", 0))

        def run_next(i):
            nonlocal token
            s = state[i]
            s["msg"], token = next_latent(i, s["hidden"], s["near"], s["from_core"], s["from_chip"], token)
            sent = lax.ppermute(s["msg"], "pp", down)
            over = swap(sent, "x", 1)
            s["msgs"] = (sent, over, swap(sent, "core", 1), swap(over, "core", 1))

        def in_order(flag, mine, other):
            return jnp.where(flag == 0, jnp.stack([mine, other]), jnp.stack([other, mine]))

        def second_stage(lens, msgs, own, other):
            pairs = [in_order(chip, msgs[0], msgs[1]), in_order(chip, msgs[2], msgs[3])]
            whole = in_order(core, *pairs)
            latent = whole[:, :, :half].reshape(2, seq, msg_cols)
            row = whole[:, :, half:].reshape(2, 2, 16 * msg_cols)[..., :width]
            row = row[:, 0] + row[:, 1]
            return last_attention(lens, latent, row), row, latent[..., :kv_rank], latent[..., kv_rank:kv_rank + rope]

        def first_stage(lens, msgs, own, other):
            cut = lambda first, last: in_order(core, own[:, first:last], other[:, first:last])
            return (jnp.zeros((2, heads * v_head), BF16), jnp.zeros((2, width), BF16),
                    cut(q_rank, q_rank + kv_rank), cut(q_rank + kv_rank, q_rank + kv_rank + rope))

        run = dict(down=run_down, att=run_att, suma=run_suma, res=run_res, mlp=run_mlp, summ=run_summ, next=run_next)
        for kind, i in ORDER:
            run[kind](i)
        ends = []
        for i, s in enumerate(state):
            lens = lax.slice_in_dim(seq_len, 2 * i, 2 * i + 2)
            ends.append(lax.cond(stage == pp_size - 1, second_stage, first_stage, lens, s["msgs"], s["own"], s["other"]))

        outs, hidden, cached, turned = (jnp.concatenate(group, axis=0) for group in zip(*ends))

        def add(base, part):
            for axis in ("core", "x"):
                part = (part.astype(F32) + swap(part, axis, 1).astype(F32)).astype(BF16)
            return (base.astype(F32) + scale * part.astype(F32)).astype(BF16)

        hidden = add(hidden, rows_matmul(outs, wo_part))
        hidden = add(hidden, rows_mlp(rms_norm(hidden, norm_mlp[0])))
        final = rms_norm(hidden, norm_final)
        final = jnp.where(stage == pp_size - 1, final, lax.ppermute(final, "pp", up))
        return cached[None], turned[None], final

    tp = ("x", "core")
    weight_specs = (P("pp", None), P("pp", None, None), P("pp", None), P("pp", None, tp), P("pp", None, None), P("pp", None),
                    P("pp", None, tp), P("pp", tp, None), P("pp", None), P("pp", None, tp), P("pp", None, tp), P("pp", tp, None))
    in_specs = (P("dp", None, None), P("dp")) + weight_specs + (P(None),)
    out_specs = (P("pp", "dp", None, None), P("pp", "dp", None, None), P("dp", None))
    return jax.shard_map(program, mesh=grid, in_specs=in_specs, out_specs=out_specs, check_vma=False)
```

time: 6380 us -> 1970 us (0.31)
  waiting for transfers between devices: 4270 us -> 611 us
  matrix products: 1520 us -> 0 us
  Pallas kernels: 0 us -> 1180 us
  other arithmetic: 396 us -> 20 us
  local copies, waits for them, and re-layouts: 133 us -> 15.6 us
  starting transfers between devices: 35.9 us -> 115 us
    psum x7 -> x0, waiting for transfers between devices: 2520 us -> none  [the longest x3 1250 us: layer_step(): hidden = residual(hidden, lax.psum(mlp_part, 'tp'), res_scale)]
    dot_general x30 -> x0, matrix products: 1360 us -> none  [the longest x24 1190 us: matmul_f32(): return jnp.dot(act_in, weight, preferred_element_type=jnp.float32)]
    pallas_call x0 -> x30, Pallas kernels: none -> 1180 us  [call(): pl.pallas_call(kernel, grid_spec=pltpu.PrefetchScalarGridSpec(num_scalar_...]
    ppermute x3 -> x56, waiting for transfers between devices: 1570 us -> 611 us  [the longest x48 422 us: swap(): lax.ppermute(value, ('pp', axis), [(2 * stage_of, 2 * stage_of + 1), (2 *...]
    all_gather x3 -> x0, waiting for transfers between devices: 181 us -> none  [layer_step(): lax.all_gather(joined, 'tp', axis=0, tiled=True)]
    convert_element_type x33 -> x5, other arithmetic: 181 us -> 2.68 us  [the longest x2 1.84 us: add(): part = (part.astype(F32) + swap(part, axis, 1).astype(F32)).astype(BF16)]
    reduce_sum x12 -> x2, other arithmetic: 169 us -> 0.44 us  [rms_wide(): inv = lax.rsqrt(jnp.mean(wide * wide, axis=-1, keepdims=True) + RMS_EPS)]
    sub x3 -> x0, matrix products: 164 us -> none  [attend(): jax.nn.softmax(jnp.where(allowed, scores, -1e+30), axis=-1)]
  transfers between devices with their start and end apart: 13 -> 56, of which waited for: 13 -> 13; matrix products, arithmetic and copies ran while one was open for 1% -> 1% of each run, Pallas kernels for 0% -> 40%
where the time goes in v1:
time: 1970 us; the launch traced here: 1960 us
  Pallas kernels  1180 us (60%)
  waiting for transfers between devices  611 us (31%)
  starting transfers between devices  115 us (6%)
  other arithmetic  20 us (1%)
    pallas_call x30, Pallas kernels, call(): pl.pallas_call(kernel, grid_spec=pltpu.PrefetchScalarGridSpec(num_scalar_...  1180 us
    ppermute x48, waiting for transfers between devices, swap(): lax.ppermute(value, ('pp', axis), [(2 * stage_of, 2 * stage_of + 1), (2 *...  422 us
    ppermute x1, waiting for transfers between devices, program(): lax.ppermute(final, 'pp', up)  170 us
    ppermute x48, starting transfers between devices, swap(): lax.ppermute(value, ('pp', axis), [(2 * stage_of, 2 * stage_of + 1), (2 *...  96.1 us
  transfers between devices with their start and end apart: 56, of which 13 were waited for; matrix products, arithmetic and copies ran while one was open for 1% of the time, Pallas kernels for 40%

profile of v1, /device:TPU:0, one launch (start us, length us, event | category | flops | bytes accessed | tf_op | source)
XLA Modules:
  0.0 1955.3 jit_solution(3796490499051248283)
XLA Ops:
  3.2 23.3 %shard_map.166 = (bf16[512,2176]{1,0:T(8,128)(2,1)S(1)}, f32[8,128]{1,0:T(8,128)}) custom-call(s32[2]{0:T(128)} %pad_add_fusion.info, bf16[4096,6144]{1,0:T(8,128)(2,1)} %bitcast.139, bf16[1,6144]{1,0:T(2,128)(2,1)} %g_attn.7, bf16[6144,1536]{1,0:T(8,128)(2,1)} %bitcast.147, bf16[1,1536]{1,0:T(2,128)(2,1)} %g_q.7, bf16[576,6144]{1,0:T(8,128)(2,1)} %bitcast.171, ...), custom_call_target="tpu_custom_call" | custom-call | flops 13287555072 | bytes 33030144 | tf_op jit(solution)/shard_map/pallas_call | solution.py:66
  42.0 93.0 %shard_map.167 = (bf16[512,6144]{1,0:T(8,128)(2,1)}, bf16[512,6144]{1,0:T(8,128)(2,1)}, f32[8,128]{1,0:T(8,128)}) custom-call(s32[4]{0:T(128)} %get-tuple-element.454.info, bf16[512,2176]{1,0:T(8,128)(2,1)S(1)} %get-tuple-element.294.own_hbm, bf16[512,2176]{1,0:T(8,128)(2,1)} %collective-permute-done.other_hbm, bf16[1536,3072]{1,0:T(8,128)(2,1)} %bitcast.155, ...), custom_call_target="tpu_custom_call" | custom-call | flops 46170898432 | bytes 51380224 | tf_op jit(solution)/shard_map/pallas_call | solution.py:66
  137.8 23.2 %shard_map.168 = (bf16[512,2176]{1,0:T(8,128)(2,1)S(1)}, f32[8,128]{1,0:T(8,128)}) custom-call(s32[2]{0:T(128)} %pad_add_fusion.5.info, bf16[4096,6144]{1,0:T(8,128)(2,1)} %bitcast.140, bf16[1,6144]{1,0:T(2,128)(2,1)S(1)} %copy-done.10, bf16[6144,1536]{1,0:T(8,128)(2,1)} %bitcast.148, bf16[1,1536]{1,0:T(2,128)(2,1)S(1)} %copy-done.20, ...), custom_call_target="tpu_custom_call" | custom-call | flops 13287555072 | bytes 33030144 | tf_op jit(solution)/shard_map/pallas_call | solution.py:66
  168.7 92.9 %shard_map.170 = (bf16[512,6144]{1,0:T(8,128)(2,1)}, bf16[512,6144]{1,0:T(8,128)(2,1)}, f32[8,128]{1,0:T(8,128)}) custom-call(s32[4]{0:T(128)} %get-tuple-element.456.info, bf16[512,2176]{1,0:T(8,128)(2,1)S(1)} %get-tuple-element.301.own_hbm, bf16[512,2176]{1,0:T(8,128)(2,1)} %collective-permute-done.3.other_hbm, bf16[1536,3072]{1,0:T(8,128)(2,1)} %bitcast.156, ...), custom_call_target="tpu_custom_call" | custom-call | flops 46170898432 | bytes 51380224 | tf_op jit(solution)/shard_map/pallas_call | solution.py:66
  269.1 23.2 %shard_map.171 = (bf16[512,2176]{1,0:T(8,128)(2,1)S(1)}, f32[8,128]{1,0:T(8,128)}) custom-call(s32[2]{0:T(128)} %pad_add_fusion.7.info, bf16[4096,6144]{1,0:T(8,128)(2,1)} %bitcast.141, bf16[1,6144]{1,0:T(2,128)(2,1)S(1)} %copy-done.10, bf16[6144,1536]{1,0:T(8,128)(2,1)} %bitcast.149, bf16[1,1536]{1,0:T(2,128)(2,1)S(1)} %copy-done.20, ...), custom_call_target="tpu_custom_call" | custom-call | flops 13287555072 | bytes 33030144 | tf_op jit(solution)/shard_map/pallas_call | solution.py:66
  302.0 36.2 %collective-permute-done.2.chip_ref = bf16[256,6144]{1,0:T(8,128)(2,1)} collective-permute-done((bf16[256,6144]{1,0:T(8,128)(2,1)}, bf16[256,6144]{1,0:T(8,128)(2,1)}, u32[]{:S(2)}, u32[]{:S(2)}) %collective-permute-start.2) | collective-permute-done | bytes 3145760 | tf_op jit(solution)/shard_map/ppermute | solution.py:456
  351.4 92.8 %shard_map.174 = (bf16[512,6144]{1,0:T(8,128)(2,1)}, bf16[512,6144]{1,0:T(8,128)(2,1)}, f32[8,128]{1,0:T(8,128)}) custom-call(s32[4]{0:T(128)} %get-tuple-element.455.info, bf16[512,2176]{1,0:T(8,128)(2,1)S(1)} %get-tuple-element.310.own_hbm, bf16[512,2176]{1,0:T(8,128)(2,1)} %collective-permute-done.8.other_hbm, bf16[1536,3072]{1,0:T(8,128)(2,1)} %bitcast.157, ...), custom_call_target="tpu_custom_call" | custom-call | flops 46170898432 | bytes 51380224 | tf_op jit(solution)/shard_map/pallas_call | solution.py:66
  444.2 23.3 %shard_map.175 = (bf16[512,2176]{1,0:T(8,128)(2,1)S(1)}, f32[8,128]{1,0:T(8,128)}) custom-call(s32[2]{0:T(128)} %pad_add_fusion.11.info, bf16[4096,6144]{1,0:T(8,128)(2,1)} %bitcast.143, bf16[1,6144]{1,0:T(2,128)(2,1)S(1)} %copy-done.10, bf16[6144,1536]{1,0:T(8,128)(2,1)} %bitcast.150, bf16[1,1536]{1,0:T(2,128)(2,1)S(1)} %copy-done.20, ...), custom_call_target="tpu_custom_call" | custom-call | flops 13287555072 | bytes 33030144 | tf_op jit(solution)/shard_map/pallas_call | solution.py:66
  489.7 93.1 %shard_map.177 = (bf16[512,6144]{1,0:T(8,128)(2,1)}, bf16[512,6144]{1,0:T(8,128)(2,1)}, f32[8,128]{1,0:T(8,128)}) custom-call(s32[4]{0:T(128)} %get-tuple-element.393.info, bf16[512,2176]{1,0:T(8,128)(2,1)S(1)} %get-tuple-element.315.own_hbm, bf16[512,2176]{1,0:T(8,128)(2,1)} %collective-permute-done.10.other_hbm, bf16[1536,3072]{1,0:T(8,128)(2,1)} %bitcast.158, ...), custom_call_target="tpu_custom_call" | custom-call | flops 46170898432 | bytes 51380224 | tf_op jit(solution)/shard_map/pallas_call | solution.py:66
  595.9 131.4 %shard_map.179 = (bf16[512,6144]{1,0:T(8,128)(2,1)}, bf16[512,6144]{1,0:T(8,128)(2,1)}, f32[8,128]{1,0:T(8,128)}) custom-call(s32[2]{0:T(128)} %pad_add_fusion.8.info, bf16[256,6144]{1,0:T(8,128)(2,1)} %get-tuple-element.309.m0, bf16[256,6144]{1,0:T(8,128)(2,1)} %collective-permute-done.5.m1, bf16[256,6144]{1,0:T(8,128)(2,1)} %collective-permute-done.6.m2, ...), custom_call_target="tpu_custom_call" | custom-call | flops 115964116992 | bytes 138412032 | tf_op jit(solution)/shard_map/pallas_call | solution.py:66
  745.3 131.5 %shard_map.182 = (bf16[512,6144]{1,0:T(8,128)(2,1)}, bf16[512,6144]{1,0:T(8,128)(2,1)}, f32[8,128]{1,0:T(8,128)}) custom-call(s32[2]{0:T(128)} %pad_add_fusion.8.info, bf16[256,6144]{1,0:T(8,128)(2,1)} %get-tuple-element.323.m0, bf16[256,6144]{1,0:T(8,128)(2,1)} %collective-permute-done.13.m1, bf16[256,6144]{1,0:T(8,128)(2,1)} %collective-permute-done.14.m2, ...), custom_call_target="tpu_custom_call" | custom-call | flops 115964116992 | bytes 138412032 | tf_op jit(solution)/shard_map/pallas_call | solution.py:66
  886.6 65.4 %collective-permute-done.22.m1 = bf16[256,6144]{1,0:T(8,128)(2,1)} collective-permute-done((bf16[256,6144]{1,0:T(8,128)(2,1)}, bf16[256,6144]{1,0:T(8,128)(2,1)}, u32[]{:S(2)}, u32[]{:S(2)}) %collective-permute-start.22) | collective-permute-done | bytes 3145760 | tf_op jit(solution)/shard_map/ppermute | solution.py:456
  960.4 58.4 %collective-permute-done.26.chip_ref = bf16[256,6144]{1,0:T(8,128)(2,1)S(1)} collective-permute-done((bf16[256,6144]{1,0:T(8,128)(2,1)}, bf16[256,6144]{1,0:T(8,128)(2,1)S(1)}, u32[]{:S(2)}, u32[]{:S(2)}) %collective-permute-start.26) | collective-permute-done | bytes 3145760 | tf_op jit(solution)/shard_map/ppermute | solution.py:456
  1034.4 131.2 %shard_map.186 = (bf16[512,6144]{1,0:T(8,128)(2,1)}, bf16[512,6144]{1,0:T(8,128)(2,1)}, f32[8,128]{1,0:T(8,128)}) custom-call(s32[2]{0:T(128)} %pad_add_fusion.8.info, bf16[256,6144]{1,0:T(8,128)(2,1)} %get-tuple-element.332.m0, bf16[256,6144]{1,0:T(8,128)(2,1)} %collective-permute-done.22.m1, bf16[256,6144]{1,0:T(8,128)(2,1)} %collective-permute-done.23.m2, ...), custom_call_target="tpu_custom_call" | custom-call | flops 115964116992 | bytes 138412032 | tf_op jit(solution)/shard_map/pallas_call | solution.py:66
  1186.5 54.2 %collective-permute-done.32.m1 = bf16[256,6144]{1,0:T(8,128)(2,1)} collective-permute-done((bf16[256,6144]{1,0:T(8,128)(2,1)}, bf16[256,6144]{1,0:T(8,128)(2,1)}, u32[]{:S(2)}, u32[]{:S(2)}) %collective-permute-start.32) | collective-permute-done | bytes 3145760 | tf_op jit(solution)/shard_map/ppermute | solution.py:456
  1243.9 63.8 %collective-permute-done.18.chip_ref = bf16[256,6144]{1,0:T(8,128)(2,1)} collective-permute-done((bf16[256,6144]{1,0:T(8,128)(2,1)}, bf16[256,6144]{1,0:T(8,128)(2,1)}, u32[]{:S(2)}, u32[]{:S(2)}) %collective-permute-start.18) | collective-permute-done | bytes 3145760 | tf_op jit(solution)/shard_map/ppermute | solution.py:456
  1327.8 131.3 %shard_map.189 = (bf16[512,6144]{1,0:T(8,128)(2,1)}, bf16[512,6144]{1,0:T(8,128)(2,1)}, f32[8,128]{1,0:T(8,128)}) custom-call(s32[2]{0:T(128)} %pad_add_fusion.8.info, bf16[256,6144]{1,0:T(8,128)(2,1)} %get-tuple-element.344.m0, bf16[256,6144]{1,0:T(8,128)(2,1)} %collective-permute-done.32.m1, bf16[256,6144]{1,0:T(8,128)(2,1)} %collective-permute-done.33.m2, ...), custom_call_target="tpu_custom_call" | custom-call | flops 115964116992 | bytes 138412032 | tf_op jit(solution)/shard_map/pallas_call | solution.py:66
  1466.9 67.3 %collective-permute-done.31.chip_ref = bf16[256,6144]{1,0:T(8,128)(2,1)} collective-permute-done((bf16[256,6144]{1,0:T(8,128)(2,1)}, bf16[256,6144]{1,0:T(8,128)(2,1)}, u32[]{:S(2)}, u32[]{:S(2)}) %collective-permute-start.31) | collective-permute-done | bytes 3145760 | tf_op jit(solution)/shard_map/ppermute | solution.py:456
  1534.2 15.0 shard_map.190
  1574.6 27.0 %collective-permute-done.40.chip_ref = bf16[256,6144]{1,0:T(8,128)(2,1)} collective-permute-done((bf16[256,6144]{1,0:T(8,128)(2,1)}, bf16[256,6144]{1,0:T(8,128)(2,1)}, u32[]{:S(2)}, u32[]{:S(2)}) %collective-permute-start.40) | collective-permute-done | bytes 3145760 | tf_op jit(solution)/shard_map/ppermute | solution.py:456
  1618.6 50.0 %collective-permute-done.46.chip_ref = bf16[256,6144]{1,0:T(8,128)(2,1)} collective-permute-done((bf16[256,6144]{1,0:T(8,128)(2,1)}, bf16[256,6144]{1,0:T(8,128)(2,1)}, u32[]{:S(2)}, u32[]{:S(2)}) %collective-permute-start.46) | collective-permute-done | bytes 3145760 | tf_op jit(solution)/shard_map/ppermute | solution.py:456
  1668.6 15.2 shard_map.193
  1732.9 42.3 %shard_map.195 = bf16[8,6144]{1,0:T(8,128)(2,1)} custom-call(s32[1]{0:T(128)} %bitcast.44.info, bf16[8,6144]{1,0:T(8,128)(2,1)} %fusion.47.rows_ref, bf16[6144,3072]{1,0:T(8,128)(2,1)} %bitcast.180, bf16[6144,3072]{1,0:T(8,128)(2,1)} %bitcast.185, bf16[3072,6144]{1,0:T(8,128)(2,1)} %bitcast.190), custom_call_target="tpu_custom_call" | custom-call | flops 905969664 | bytes 113246208 | tf_op jit(solution)/shard_map/pallas_call | solution.py:66
  1783.7 170.4 %collective-permute-done.55 = bf16[8,6144]{1,0:T(8,128)(2,1)S(1)} collective-permute-done((bf16[8,6144]{1,0:T(8,128)(2,1)S(1)}, bf16[8,6144]{1,0:T(8,128)(2,1)S(1)}, u32[]{:S(2)}, u32[]{:S(2)}) %collective-permute-start.55) | collective-permute-done | bytes 98336 | tf_op jit(solution)/shard_map/ppermute | solution.py:530
  (244 shorter events, 301.2 us)
Async XLA Ops:
  300.0 174.6 %collective-permute-start.11 = (bf16[256,6144]{1,0:T(8,128)(2,1)}, bf16[256,6144]{1,0:T(8,128)(2,1)}, u32[]{:S(2)}, u32[]{:S(2)}) collective-permute-start(bf16[256,6144]{1,0:T(8,128)(2,1)} %get-tuple-element.316), channel_id=1, source_target_pairs={{0,2},{2,0},{1,3},{3,1}} | collective-permute-start | bytes 9437192 | tf_op jit(solution)/shard_map/ppermute | solution.py:456
  346.9 140.7 %collective-permute-start.5 = (bf16[256,6144]{1,0:T(8,128)(2,1)}, bf16[256,6144]{1,0:T(8,128)(2,1)}, u32[]{:S(2)}, u32[]{:S(2)}) collective-permute-start(bf16[256,6144]{1,0:T(8,128)(2,1)} %get-tuple-element.309.m0), channel_id=1, source_target_pairs={{0,2},{2,0},{1,3},{3,1}} | collective-permute-start | bytes 9437192 | tf_op jit(solution)/shard_map/ppermute | solution.py:456
  469.5 113.2 %collective-permute-start.9 = (bf16[512,6144]{1,0:T(8,128)(2,1)}, bf16[512,6144]{1,0:T(8,128)(2,1)}, u32[]{:S(2)}, u32[]{:S(2)}) collective-permute-start(bf16[512,6144]{1,0:T(8,128)(2,1)} %get-tuple-element.313), channel_id=1, source_target_pairs={{0,1},{1,0},{2,3},{3,2}} | collective-permute-start | bytes 18874376 | tf_op jit(solution)/shard_map/ppermute | solution.py:456
  472.6 117.7 %collective-permute-start.6 = (bf16[256,6144]{1,0:T(8,128)(2,1)}, bf16[256,6144]{1,0:T(8,128)(2,1)}, u32[]{:S(2)}, u32[]{:S(2)}) collective-permute-start(bf16[256,6144]{1,0:T(8,128)(2,1)} %get-tuple-element.309.m0), channel_id=1, source_target_pairs={{0,1},{1,0},{2,3},{3,2}} | collective-permute-start | bytes 9437192 | tf_op jit(solution)/shard_map/ppermute | solution.py:456
  483.3 110.6 %collective-permute-start.13 = (bf16[256,6144]{1,0:T(8,128)(2,1)}, bf16[256,6144]{1,0:T(8,128)(2,1)}, u32[]{:S(2)}, u32[]{:S(2)}) collective-permute-start(bf16[256,6144]{1,0:T(8,128)(2,1)} %get-tuple-element.323.m0), channel_id=1, source_target_pairs={{0,2},{2,0},{1,3},{3,1}} | collective-permute-start | bytes 9437192 | tf_op jit(solution)/shard_map/ppermute | solution.py:456
  485.3 260.1 %collective-permute-start.14 = (bf16[256,6144]{1,0:T(8,128)(2,1)}, bf16[256,6144]{1,0:T(8,128)(2,1)}, u32[]{:S(2)}, u32[]{:S(2)}) collective-permute-start(bf16[256,6144]{1,0:T(8,128)(2,1)} %get-tuple-element.323.m0), channel_id=1, source_target_pairs={{0,1},{1,0},{2,3},{3,2}} | collective-permute-start | bytes 9437192 | tf_op jit(solution)/shard_map/ppermute | solution.py:456
  487.7 108.2 %collective-permute-start.7 = (bf16[256,6144]{1,0:T(8,128)(2,1)}, bf16[256,6144]{1,0:T(8,128)(2,1)}, u32[]{:S(2)}, u32[]{:S(2)}) collective-permute-start(bf16[256,6144]{1,0:T(8,128)(2,1)} %collective-permute-done.5.m1), channel_id=1, source_target_pairs={{0,1},{1,0},{2,3},{3,2}} | collective-permute-start | bytes 9437192 | tf_op jit(solution)/shard_map/ppermute | solution.py:456
  582.7 157.5 %collective-permute-start.16 = (bf16[512,6144]{1,0:T(8,128)(2,1)}, bf16[512,6144]{1,0:T(8,128)(2,1)}, u32[]{:S(2)}, u32[]{:S(2)}) collective-permute-start(bf16[512,6144]{1,0:T(8,128)(2,1)} %get-tuple-element.325), channel_id=1, source_target_pairs={{0,1},{1,0},{2,3},{3,2}} | collective-permute-start | bytes 18874376 | tf_op jit(solution)/shard_map/ppermute | solution.py:456
  590.3 139.5 %collective-permute-start.17 = (bf16[256,6144]{1,0:T(8,128)(2,1)}, bf16[256,6144]{1,0:T(8,128)(2,1)S(1)}, u32[]{:S(2)}, u32[]{:S(2)}) collective-permute-start(bf16[256,6144]{1,0:T(8,128)(2,1)} %get-tuple-element.326), channel_id=1, source_target_pairs={{0,2},{2,0},{1,3},{3,1}} | collective-permute-start | bytes 9437192 | tf_op jit(solution)/shard_map/ppermute | solution.py:456
  593.9 151.4 %collective-permute-start.15 = (bf16[256,6144]{1,0:T(8,128)(2,1)}, bf16[256,6144]{1,0:T(8,128)(2,1)}, u32[]{:S(2)}, u32[]{:S(2)}) collective-permute-start(bf16[256,6144]{1,0:T(8,128)(2,1)} %collective-permute-done.13.m1), channel_id=1, source_target_pairs={{0,1},{1,0},{2,3},{3,2}} | collective-permute-start | bytes 9437192 | tf_op jit(solution)/shard_map/ppermute | solution.py:456
  727.3 226.6 %collective-permute-start.12 = (bf16[512,6144]{1,0:T(8,128)(2,1)}, bf16[512,6144]{1,0:T(8,128)(2,1)}, u32[]{:S(2)}, u32[]{:S(2)}) collective-permute-start(bf16[512,6144]{1,0:T(8,128)(2,1)} %get-tuple-element.322), channel_id=1, source_target_pairs={{0,1},{1,0},{2,3},{3,2}} | collective-permute-start | bytes 18874376 | tf_op jit(solution)/shard_map/ppermute | solution.py:456
  876.8 152.4 %collective-permute-start.25 = (bf16[512,6144]{1,0:T(8,128)(2,1)}, bf16[512,6144]{1,0:T(8,128)(2,1)}, u32[]{:S(2)}, u32[]{:S(2)}) collective-permute-start(bf16[512,6144]{1,0:T(8,128)(2,1)} %get-tuple-element.334), channel_id=1, source_target_pairs={{0,1},{1,0},{2,3},{3,2}} | collective-permute-start | bytes 18874376 | tf_op jit(solution)/shard_map/ppermute | solution.py:456
  881.0 137.8 %collective-permute-start.26 = (bf16[256,6144]{1,0:T(8,128)(2,1)}, bf16[256,6144]{1,0:T(8,128)(2,1)S(1)}, u32[]{:S(2)}, u32[]{:S(2)}) collective-permute-start(bf16[256,6144]{1,0:T(8,128)(2,1)} %get-tuple-element.335), channel_id=1, source_target_pairs={{0,2},{2,0},{1,3},{3,1}} | collective-permute-start | bytes 9437192 | tf_op jit(solution)/shard_map/ppermute | solution.py:456
  884.6 149.7 %collective-permute-start.23 = (bf16[256,6144]{1,0:T(8,128)(2,1)}, bf16[256,6144]{1,0:T(8,128)(2,1)}, u32[]{:S(2)}, u32[]{:S(2)}) collective-permute-start(bf16[256,6144]{1,0:T(8,128)(2,1)} %get-tuple-element.332.m0), channel_id=1, source_target_pairs={{0,1},{1,0},{2,3},{3,2}} | collective-permute-start | bytes 9437192 | tf_op jit(solution)/shard_map/ppermute | solution.py:456
  953.9 290.0 %collective-permute-start.20 = (bf16[576,6144]{1,0:T(8,128)(2,1)}, bf16[576,6144]{1,0:T(8,128)(2,1)}, u32[]{:S(2)}, u32[]{:S(2)}) collective-permute-start(bf16[576,6144]{1,0:T(8,128)(2,1)} %bitcast.175), channel_id=1, source_target_pairs={{4,0},{5,1},{6,2},{7,3}} | collective-permute-start | bytes 21233672 | tf_op jit(solution)/shard_map/ppermute | solution.py:341
  1165.6 157.0 %collective-permute-start.35 = (bf16[512,6144]{1,0:T(8,128)(2,1)}, bf16[512,6144]{1,0:T(8,128)(2,1)}, u32[]{:S(2)}, u32[]{:S(2)}) collective-permute-start(bf16[512,6144]{1,0:T(8,128)(2,1)} %get-tuple-element.346), channel_id=1, source_target_pairs={{0,1},{1,0},{2,3},{3,2}} | collective-permute-start | bytes 18874376 | tf_op jit(solution)/shard_map/ppermute | solution.py:456
  1169.8 137.9 %collective-permute-start.18 = (bf16[256,6144]{1,0:T(8,128)(2,1)}, bf16[256,6144]{1,0:T(8,128)(2,1)}, u32[]{:S(2)}, u32[]{:S(2)}) collective-permute-start(bf16[256,6144]{1,0:T(8,128)(2,1)} %get-tuple-element.331), channel_id=1, source_target_pairs={{0,2},{2,0},{1,3},{3,1}} | collective-permute-start | bytes 9437192 | tf_op jit(solution)/shard_map/ppermute | solution.py:456
  1184.6 143.1 %collective-permute-start.33 = (bf16[256,6144]{1,0:T(8,128)(2,1)}, bf16[256,6144]{1,0:T(8,128)(2,1)}, u32[]{:S(2)}, u32[]{:S(2)}) collective-permute-start(bf16[256,6144]{1,0:T(8,128)(2,1)} %get-tuple-element.344.m0), channel_id=1, source_target_pairs={{0,1},{1,0},{2,3},{3,2}} | collective-permute-start | bytes 9437192 | tf_op jit(solution)/shard_map/ppermute | solution.py:456
  1463.2 138.4 %collective-permute-start.40 = (bf16[256,6144]{1,0:T(8,128)(2,1)}, bf16[256,6144]{1,0:T(8,128)(2,1)}, u32[]{:S(2)}, u32[]{:S(2)}) collective-permute-start(bf16[256,6144]{1,0:T(8,128)(2,1)} %get-tuple-element.353), channel_id=1, source_target_pairs={{0,2},{2,0},{1,3},{3,1}} | collective-permute-start | bytes 9437192 | tf_op jit(solution)/shard_map/ppermute | solution.py:456
  1554.4 114.2 %collective-permute-start.46 = (bf16[256,6144]{1,0:T(8,128)(2,1)}, bf16[256,6144]{1,0:T(8,128)(2,1)}, u32[]{:S(2)}, u32[]{:S(2)}) collective-permute-start(bf16[256,6144]{1,0:T(8,128)(2,1)} %get-tuple-element.361), channel_id=1, source_target_pairs={{0,2},{2,0},{1,3},{3,1}} | collective-permute-start | bytes 9437192 | tf_op jit(solution)/shard_map/ppermute | solution.py:456
  1564.6 122.5 %collective-permute-start.28 = (bf16[272,640]{1,0:T(8,128)(2,1)S(1)}, bf16[272,640]{1,0:T(8,128)(2,1)S(1)}, u32[]{:S(2)}, u32[]{:S(2)}) collective-permute-start(bf16[272,640]{1,0:T(8,128)(2,1)S(1)} %collective-permute-done.27), channel_id=1, source_target_pairs={{4,6},{6,4},{5,7},{7,5}} | collective-permute-start | bytes 1044488 | tf_op jit(solution)/shard_map/ppermute | solution.py:456
  1565.3 124.0 %collective-permute-start.29 = (bf16[272,640]{1,0:T(8,128)(2,1)S(1)}, bf16[272,640]{1,0:T(8,128)(2,1)S(1)}, u32[]{:S(2)}, u32[]{:S(2)}) collective-permute-start(bf16[272,640]{1,0:T(8,128)(2,1)S(1)} %collective-permute-done.27), channel_id=1, source_target_pairs={{4,5},{5,4},{6,7},{7,6}} | collective-permute-start | bytes 1044488 | tf_op jit(solution)/shard_map/ppermute | solution.py:456
  1566.0 119.8 %collective-permute-start.36 = (bf16[272,640]{1,0:T(8,128)(2,1)S(1)}, bf16[272,640]{1,0:T(8,128)(2,1)S(1)}, u32[]{:S(2)}, u32[]{:S(2)}) collective-permute-start(bf16[272,640]{1,0:T(8,128)(2,1)S(1)} %copy-done.43), channel_id=1, source_target_pairs={{0,4},{1,5},{2,6},{3,7}} | collective-permute-start | bytes 1044488 | tf_op jit(solution)/shard_map/ppermute | solution.py:492
  1781.5 172.6 %collective-permute-start.55 = (bf16[8,6144]{1,0:T(8,128)(2,1)S(1)}, bf16[8,6144]{1,0:T(8,128)(2,1)S(1)}, u32[]{:S(2)}, u32[]{:S(2)}) collective-permute-start(bf16[8,6144]{1,0:T(8,128)(2,1)S(1)} %fusion.44), channel_id=1, source_target_pairs={{4,0},{5,1},{6,2},{7,3}} | collective-permute-start | bytes 294920 | tf_op jit(solution)/shard_map/ppermute | solution.py:530
  (65 other events, 3665.7 us)

commit v2 on v1

--- a/solution.py
+++ b/solution.py
@@ -2,6 +2,7 @@
 import math
 import jax
 import jax.numpy as jnp
+import numpy as np
 from jax import lax
 from jax.experimental import pallas as pl
 from jax.experimental.pallas import tpu as pltpu
@@ -12,6 +13,9 @@
 SCALE_DEPTH = 1.4
 BF16, F32 = jnp.bfloat16, jnp.float32
 ROWS = 128
+TALL = 256
+WIDE = 256
+SHORT = 32
 HEAD_BLOCK = 4
 OUT_COLS = 768
 ACT_COLS = 256
@@ -49,10 +53,11 @@
 
 
 def rope_tables(seq, rope):
-    inv_freq = ROPE_BASE ** (-2.0 * jnp.arange(rope // 2, dtype=F32) / rope)
-    angle = jnp.arange(seq, dtype=F32)[:, None] * inv_freq[None, :]
-    cos_t, sin_t = jnp.cos(angle), jnp.sin(angle)
-    return jnp.concatenate([cos_t, cos_t], axis=-1), jnp.concatenate([-sin_t, sin_t], axis=-1)
+    inv_freq = (ROPE_BASE ** (-2.0 * np.arange(rope // 2) / rope)).astype(np.float32)
+    angle = (np.arange(seq, dtype=np.float32)[:, None] * inv_freq[None, :]).astype(np.float64)
+    cos_t, sin_t = np.cos(angle), np.sin(angle)
+    tables = np.concatenate([cos_t, cos_t], axis=-1), np.concatenate([-sin_t, sin_t], axis=-1)
+    return tuple(jnp.asarray(table.astype(np.float32)) for table in tables)
 
 
 def apply_rope(values_in, cos_t, sin_t):
@@ -82,13 +87,14 @@
     return pl.BlockSpec(shape, lambda *_: (0,) * len(shape))
 
 
-ORDER = [
-    ("down", 0), ("att", 0), ("down", 1), ("suma", 0), ("att", 1), ("down", 2),
-    ("suma", 1), ("res", 0), ("att", 2), ("down", 3), ("res", 1), ("att", 3),
-    ("suma", 2), ("mlp", 0), ("res", 2), ("suma", 3), ("mlp", 1), ("summ", 0),
-    ("res", 3), ("summ", 1), ("mlp", 2), ("next", 0), ("summ", 2), ("mlp", 3),
-    ("next", 1), ("summ", 3), ("next", 2), ("next", 3),
+NAMES = [
+    "down_0", "down_1", "att_0", "down_2", "suma_0", "att_1",
+    "down_3", "suma_1", "res_0", "att_2", "res_1", "att_3",
+    "suma_2", "mlp_0", "res_2", "suma_3", "mlp_1", "summ_0",
+    "res_3", "summ_1", "mlp_2", "next_0", "summ_2", "mlpx_3",
+    "next_1", "next_2", "summ_3", "mlpo_3", "next_3",
 ]
+ORDER = [(name[:-2], int(name[-1])) for name in NAMES]
 
 
 def down_kernel(dims, info, x_ref, g_attn, wq_ref, g_q, wkv_hbm, g_kv, cos_ref, sin_ref, _, joined_ref, token_ref,
@@ -130,74 +136,133 @@
 
 
 def attention_kernel(dims, info, own_hbm, other_hbm, wq_ref, wkv_ref, wo_ref, cos_ref, sin_ref, _, near_ref, far_ref, token_ref,
-                     joined, outs, sems):
+                     joined, q_ref, kv_ref, bias_ref, s_ref, p_ref, outs, sems):
     q_rank, kv_rank, nope, rope, v_head, steps = dims
     step = pl.program_id(0)
     active = info[0] == 1
     qk, seq = nope + rope, joined.shape[1]
     copies = [pltpu.make_async_copy(ref, joined.at[i], sems.at[i]) for i, ref in enumerate((own_hbm, other_hbm))]
 
+    chip = info[1]
+    half = seq // 2
+    sides = near_ref, far_ref
+
+    def projections(prompt):
+        def piece(out_ref, w_ref, first, last, rows, cols):
+            out_ref[prompt, rows, cols] = dot(joined[prompt, rows, first:last], w_ref[:, cols]).astype(BF16)
+
+        for out_ref, w_ref, first, last in ((q_ref, wq_ref, 0, q_rank), (kv_ref, wkv_ref, q_rank, q_rank + kv_rank)):
+            for col in range(0, out_ref.shape[2], WIDE):
+                for row in range(0, seq, TALL):
+                    yield functools.partial(piece, out_ref, w_ref, first, last, pl.ds(row, TALL), pl.ds(col, WIDE))
+
+    def out_pieces(prompt):
+        def piece(rows):
+            sides[prompt][rows, :] = dot(outs[prompt, rows, :], wo_ref[...]).astype(BF16)
+
+        return [functools.partial(piece, pl.ds(row, TALL)) for row in range(0, seq, TALL)]
+
+    def attend(prompt, group, extra):
+        length = info[2 + prompt]
+        for first in range(0, seq, SHORT):
+            limit = jnp.minimum(lax.broadcasted_iota(jnp.int32, (SHORT, 1), 0) + first, length - 1)
+            bias_ref[pl.ds(first, SHORT), :] = jnp.where(lax.broadcasted_iota(jnp.int32, (SHORT, seq), 1) <= limit, 0.0, -1e30)
+
+        def score(head, first):
+            ends, rows, slot = first + TALL, pl.ds(first, TALL), head % 2
+            pair, inner = head // 2 * 2 * qk, head % 2 * qk
+            q_pair = q_ref[prompt, rows, pair:pair + 2 * qk]
+            q_rope = apply_rope(q_pair[:, inner + nope:inner + qk], cos_ref[rows, :], sin_ref[rows, :])
+            queries = jnp.concatenate([q_pair[:, inner:inner + nope], q_rope], axis=-1)
+            base = head * (nope + v_head)
+            keys = jnp.concatenate([kv_ref[prompt, :ends, base:base + nope], joined[prompt, :ends, q_rank + kv_rank:q_rank + kv_rank + rope]], axis=-1)
+            scores = dot_t(queries, keys) * (qk ** -0.5 * math.log2(math.e))
+            s_ref[slot, rows, :ends] = scores + bias_ref[rows, :ends]
+
+        def value(head, first):
+            ends, slot = first + TALL, head % 2
+            base = head * (nope + v_head) + nope
+            place = jnp.bitwise_xor(first // half, chip) * half + first % half
+            cols = pl.ds(pl.multiple_of((group * HEAD_BLOCK + head) * v_head, v_head), v_head)
+            outs[prompt, pl.ds(pl.multiple_of(place, TALL), TALL), cols] = dot(
+                p_ref[slot, pl.ds(first, TALL), :ends], kv_ref[prompt, :ends, base:base + v_head]).astype(BF16)
+
+        def softmax(head):
+            slot = head % 2
+            units = [(first, first // TALL * TALL + TALL) for first in range(0, seq, SHORT)]
+            tops = {}
+            for at in range(len(units) + 2):
+                if at < len(units):
+                    first, ends = units[at]
+                    tops[at] = jnp.max(s_ref[slot, pl.ds(first, SHORT), :ends], axis=-1, keepdims=True)
+                if 0 <= at - 1 < len(units):
+                    first, ends = units[at - 1]
+                    total = jnp.sum(jnp.exp2(s_ref[slot, pl.ds(first, SHORT), :ends] - tops[at - 1]), axis=-1, keepdims=True)
+                    tops[at - 1] = tops[at - 1] + jnp.log2(total)
+                if 0 <= at - 2:
+                    first, ends = units[at - 2]
+                    p_ref[slot, pl.ds(first, SHORT), :ends] = jnp.exp2(s_ref[slot, pl.ds(first, SHORT), :ends] - tops.pop(at - 2)).astype(BF16)
+                yield
+
+        rounds = HEAD_BLOCK + 2
+        for head in range(rounds):
+            work = [functools.partial(score, head, first) for first in range(0, seq, TALL)] if head < HEAD_BLOCK else []
+            work += [functools.partial(value, head - 2, first) for first in range(0, seq, TALL)] if head >= 2 else []
+            work += extra[len(extra) * head // rounds:len(extra) * (head + 1) // rounds]
+            units = softmax(head - 1) if 1 <= head <= HEAD_BLOCK else iter(())
+            for piece in work:
+                piece()
+                for _ in range(3):
+                    next(units, None)
+            for _ in units:
+                pass
+
     @pl.when((step == 0) & active)
     def _():
         copies[0].start()
         copies[1].start()
         copies[0].wait()
+        for piece in projections(0):
+            piece()
 
     @pl.when((step == 1) & active)
     def _():
         copies[1].wait()
 
-    @pl.when((step < steps) & active)
-    def _():
-        prompt = step % 2
-        length = info[2 + prompt]
-        chip = info[1]
-        q_all = dot(joined[prompt, :, :q_rank], wq_ref[...]).astype(BF16)
-        kv_all = dot(joined[prompt, :, q_rank:q_rank + kv_rank], wkv_ref[...]).astype(BF16)
-        k_rope = joined[prompt, :, q_rank + kv_rank:q_rank + kv_rank + rope]
-        cos_t, sin_t = cos_ref[...], sin_ref[...]
-        for head in range(HEAD_BLOCK):
-            q_rope = apply_rope(q_all[:, head * qk + nope:(head + 1) * qk], cos_t, sin_t)
-            queries = jnp.concatenate([q_all[:, head * qk:head * qk + nope], q_rope], axis=-1)
-            base = head * (nope + v_head)
-            keys = jnp.concatenate([kv_all[:, base:base + nope], k_rope], axis=-1)
-            values = kv_all[:, base + nope:base + nope + v_head]
-            cols = pl.ds(pl.multiple_of(((step // 2) * HEAD_BLOCK + head) * v_head, v_head), v_head)
-            for first in range(0, seq, ROWS):
-                ends = first + ROWS
-                scores = lax.dot_general(queries[first:ends], keys[:ends], (((1,), (1,)), ((), ())),
-                                         preferred_element_type=F32) * (qk ** -0.5 * math.log2(math.e))
-                limit = jnp.minimum(lax.broadcasted_iota(jnp.int32, (ROWS, 1), 0) + first, length - 1)
-                scores = jnp.where(lax.broadcasted_iota(jnp.int32, (ROWS, ends), 1) <= limit, scores, -1e30)
-                grown = jnp.exp2(scores - jnp.max(scores, axis=-1, keepdims=True))
-                probs = (grown * (1.0 / jnp.sum(grown, axis=-1, keepdims=True))).astype(BF16)
-                half = seq // 2
-                place = jnp.bitwise_xor(first // half, chip) * half + first % half
-                outs[prompt, pl.ds(pl.multiple_of(place, ROWS), ROWS), cols] = dot(probs, values[:ends]).astype(BF16)
-
-    @pl.when((step >= steps) & active)
-    def _():
-        for prompt, out_ref in enumerate((near_ref, far_ref)):
-            for first in range(0, seq, 256):
-                out_ref[pl.ds(first, 256), :] = dot(outs[prompt, pl.ds(first, 256), :], wo_ref[...]).astype(BF16)
+    for parity in range(2):
+        @pl.when((step > 0) & (step < steps) & (step % 2 == parity) & active)
+        def _():
+            attend(1 - parity, (step - 1) // 2, list(projections(parity)))
+
+    @pl.when((step == steps) & active)
+    def _():
+        attend(1, (step - 1) // 2, out_pieces(0))
+        for piece in out_pieces(1):
+            piece()
+
+    @pl.when((step > steps) & active)
+    def _():
+        for piece in out_pieces(0) + out_pieces(1):
+            piece()
 
     @pl.when(step == pl.num_programs(0) - 1)
     def _():
         token_ref[...] = jnp.zeros_like(token_ref)
 
 
-def mlp_kernel(steps, info, m0, m1, m2, m3, w1_ref, w3_ref, w2_ref, _, near_ref, far_ref, token_ref, rows_ref, act_ref, sems):
+def mlp_kernel(steps, count, info, *refs):
+    pieces, (w1_ref, w3_ref, w2_ref, _, near_ref, far_ref, token_ref, rows_ref, act_ref, sems) = refs[:count], refs[count:]
     step = pl.program_id(0)
     active = info[0] == 1
-    piece = m0.shape[0]
-    copies = [pltpu.make_async_copy(ref, rows_ref.at[pl.ds(i * piece, piece)], sems.at[i]) for i, ref in enumerate((m0, m1, m2, m3))]
+    depth = pieces[0].shape[0]
+    copies = [pltpu.make_async_copy(ref, rows_ref.at[pl.ds(i * depth, depth)], sems.at[i]) for i, ref in enumerate(pieces)]
 
     def gate(first_step):
         cols = pl.ds(pl.multiple_of(step * ACT_COLS, ACT_COLS), ACT_COLS)
-        for i in range(4):
+        for i in range(count):
             if first_step:
                 copies[i].wait()
-            rows = pl.ds(i * piece, piece)
+            rows = pl.ds(i * depth, depth)
             wide = dot(rows_ref[rows, :], w1_ref[...])
             act_ref[rows, cols] = (wide * jax.nn.sigmoid(wide) * dot(rows_ref[rows, :], w3_ref[...])).astype(BF16)
 
@@ -213,9 +278,9 @@
 
     @pl.when((step >= steps) & active)
     def _():
-        for i in range(4):
-            out_ref = near_ref if i < 2 else far_ref
-            out_ref[pl.ds((i % 2) * piece, piece), :] = dot(act_ref[pl.ds(i * piece, piece), :], w2_ref[...]).astype(BF16)
+        for i in range(count):
+            out_ref = near_ref if i < count // 2 else far_ref
+            out_ref[pl.ds(i % (count // 2) * depth, depth), :] = dot(act_ref[pl.ds(i * depth, depth), :], w2_ref[...]).astype(BF16)
 
     @pl.when(step == pl.num_programs(0) - 1)
     def _():
@@ -227,52 +292,68 @@
     token_ref[...] = jnp.zeros_like(token_ref)
 
 
-def join(scale, hidden, near, other_core, other_chip):
-    both = (near.astype(F32) + other_core.astype(F32)).astype(BF16)
-    branch = (both.astype(F32) + other_chip.astype(F32)).astype(BF16)
-    return (hidden.astype(F32) + scale * branch.astype(F32)).astype(BF16)
+def join_rows(scale, refs, gain_ref, h_ref, u_ref, rows):
+    x_ref, near_ref, core_ref, chip_ref = refs
+    count, width = x_ref.shape
+    cols, block = 256, 32
+    for first in range(0, count, block):
+        at = pl.ds(first, block)
+        squares = jnp.zeros((block, cols), F32)
+        for col in range(0, width, cols):
+            part = pl.ds(col, cols)
+            both = (near_ref[at, part].astype(F32) + core_ref[at, part].astype(F32)).astype(BF16)
+            branch = (both.astype(F32) + chip_ref[at, part].astype(F32)).astype(BF16)
+            hidden = (x_ref[at, part].astype(F32) + scale * branch.astype(F32)).astype(BF16)
+            h_ref[pl.ds(rows + first, block), part] = hidden
+            squares = squares + hidden.astype(F32) * hidden.astype(F32)
+        inv = lax.rsqrt(jnp.sum(squares, axis=-1, keepdims=True) * (1.0 / width) + RMS_EPS)
+        for col in range(0, width, cols):
+            part = pl.ds(col, cols)
+            wide = h_ref[pl.ds(rows + first, block), part].astype(F32)
+            u_ref[pl.ds(rows + first, block), part] = (wide * inv * gain_ref[:, part].astype(F32)).astype(BF16)
 
 
 def residual_kernel(scale, info, x_ref, near_ref, core_ref, chip_ref, gain, _, h_ref, m_ref, token_ref):
-    hidden = join(scale, x_ref[...], near_ref[...], core_ref[...], chip_ref[...])
-    h_ref[...] = hidden
-    m_ref[...] = rms_norm(hidden, gain[...])
+    join_rows(scale, (x_ref, near_ref, core_ref, chip_ref), gain, h_ref, m_ref, 0)
     token_ref[...] = jnp.zeros_like(token_ref)
 
 
-def next_kernel(scale, kv_rank, info, h_ref, near_ref, core_ref, chip_ref, g_attn, wkv_ref, g_kv, cos_ref, sin_ref, _,
-                msg_ref, token_ref, row_ref):
+def next_kernel(scale, kv_rank, steps, info, x_ref, near_ref, core_ref, chip_ref, g_attn, wkv_hbm, g_kv, cos_ref, sin_ref, _,
+                msg_ref, token_ref, h_ref, u_ref, wkv_ref, sem):
     step = pl.program_id(0)
-    rows = h_ref.shape[0]
-    total = rows * pl.num_programs(0)
-    hidden = join(scale, h_ref[...], near_ref[...], core_ref[...], chip_ref[...])
-    low = dot_t(rms_norm(hidden, g_attn[...]), wkv_ref[...]).astype(BF16)
-    msg_ref[pl.ds(pl.multiple_of(step * rows, rows), rows), :kv_rank] = rms_norm(low[:, :kv_rank], g_kv[...])
-    turned = apply_rope(low[:, kv_rank:], cos_ref[...], sin_ref[...])
-    msg_ref[pl.ds(pl.multiple_of(step * rows, rows), rows), kv_rank:] = jnp.concatenate([turned, jnp.zeros_like(turned)], axis=-1)
-    wanted = info[2] - 1 - info[1] * total - step * rows
-    picked = jnp.where(lax.broadcasted_iota(jnp.int32, (rows, 1), 0) == wanted, hidden.astype(F32), 0.0)
-    picked = jnp.sum(picked, axis=0, keepdims=True)
-
-    @pl.when(step == 0)
-    def _():
-        row_ref[...] = jnp.broadcast_to(picked, row_ref.shape)
-
-    @pl.when(step > 0)
-    def _():
-        row_ref[...] += jnp.broadcast_to(picked, row_ref.shape)
-
-    @pl.when(step == pl.num_programs(0) - 1)
-    def _():
-        width = msg_ref.shape[1]
-        depth = row_ref.shape[1]
+    active = info[3] == 1
+    total, width = h_ref.shape
+    count = x_ref.shape[0]
+    copy = pltpu.make_async_copy(wkv_hbm, wkv_ref, sem)
+
+    @pl.when((step == 0) & active)
+    def _():
+        copy.start()
+
+    @pl.when((step < steps) & active)
+    def _():
+        join_rows(scale, (x_ref, near_ref, core_ref, chip_ref), g_attn, h_ref, u_ref, pl.multiple_of(step * count, count))
+
+    @pl.when((step == steps) & active)
+    def _():
+        copy.wait()
+        low = dot_t(u_ref[...], wkv_ref[...]).astype(BF16)
+        msg_ref[:total, :kv_rank] = rms_norm(low[:, :kv_rank], g_kv[...])
+        turned = apply_rope(low[:, kv_rank:], cos_ref[...], sin_ref[...])
+        msg_ref[:total, kv_rank:] = jnp.concatenate([turned, jnp.zeros_like(turned)], axis=-1)
+        wanted = info[2] - 1 - info[1] * total
+        block = jnp.clip(wanted // 16, 0, total // 16 - 1) * 16
+        near = h_ref[pl.ds(pl.multiple_of(block, 16), 16), :].astype(F32)
+        here = lax.broadcasted_iota(jnp.int32, (16, 1), 0) == wanted - block
+        row = jnp.sum(jnp.where(here, near, 0.0), axis=0, keepdims=True)
+        cols = msg_ref.shape[1]
         parts = []
-        for first in range(0, depth, width):
-            part = row_ref[0:1, first:min(first + width, depth)]
-            if part.shape[1] < width:
-                part = jnp.concatenate([part, jnp.zeros((1, width - part.shape[1]), F32)], axis=-1)
+        for first in range(0, width, cols):
+            part = row[:, first:min(first + cols, width)]
+            if part.shape[1] < cols:
+                part = jnp.concatenate([part, jnp.zeros((1, cols - part.shape[1]), F32)], axis=-1)
             parts.append(part)
-        parts.append(jnp.zeros((16 - len(parts), width), F32))
+        parts.append(jnp.zeros((16 - len(parts), cols), F32))
         msg_ref[pl.ds(total, 16), :] = jnp.concatenate(parts, axis=0).astype(BF16)
 
     token_ref[...] = jnp.zeros_like(token_ref)
@@ -280,32 +361,38 @@
 
 def last_kernel(dims, info, q_ref, c_ref, wkv_ref, out_ref):
     kv_rank, nope, rope, v_head = dims
+    count = q_ref.shape[2]
+    projected = [dot(c_ref[prompt, :, :kv_rank], wkv_ref[...]).astype(BF16) for prompt in range(2)]
+    scores = []
     for prompt in range(2):
-        length = info[2 + prompt]
-        kv_all = dot(c_ref[prompt, :, :kv_rank], wkv_ref[...]).astype(BF16)
         k_rope = c_ref[prompt, :, kv_rank:kv_rank + rope]
         for head in range(HEAD_BLOCK):
             base = head * (nope + v_head)
-            keys = jnp.concatenate([kv_all[:, base:base + nope], k_rope], axis=-1)
-            query = q_ref[prompt, head]
-            scores = lax.dot_general(query, keys, (((1,), (1,)), ((), ())), preferred_element_type=F32) * (nope + rope) ** -0.5
-            scores = jnp.where(lax.broadcasted_iota(jnp.int32, scores.shape, 1) < length, scores, -1e30)
-            grown = jnp.exp(scores - jnp.max(scores, axis=-1, keepdims=True))
-            probs = (grown * (1.0 / jnp.sum(grown, axis=-1, keepdims=True))).astype(BF16)
-            out_ref[prompt, :, head * v_head:(head + 1) * v_head] = dot(probs, kv_all[:, base + nope:base + nope + v_head]).astype(BF16)
+            keys = jnp.concatenate([projected[prompt][:, base:base + nope], k_rope], axis=-1)
+            found = dot_t(q_ref[prompt, head], keys) * (nope + rope) ** -0.5
+            scores.append(jnp.where(lax.broadcasted_iota(jnp.int32, found.shape, 1) < info[2 + prompt], found, -1e30))
+    scores = jnp.concatenate(scores, axis=0)
+    grown = jnp.exp(scores - jnp.max(scores, axis=-1, keepdims=True))
+    probs = grown * (1.0 / jnp.sum(grown, axis=-1, keepdims=True))
+    for prompt in range(2):
+        for head in range(HEAD_BLOCK):
+            base = head * (nope + v_head) + nope
+            at = (prompt * HEAD_BLOCK + head) * count
+            out_ref[prompt, :, head * v_head:(head + 1) * v_head] = dot(
+                probs[at:at + count].astype(BF16), projected[prompt][:, base:base + v_head]).astype(BF16)
 
 
 def rows_kernel(info, rows_ref, w_ref, out_ref):
     out_ref[...] = dot(rows_ref[...], w_ref[...]).astype(BF16)
 
 
-def rows_mlp_kernel(steps, info, rows_ref, w1_ref, w3_ref, w2_ref, out_ref, act_ref):
+def rows_mlp_kernel(steps, act_cols, info, rows_ref, w1_ref, w3_ref, w2_ref, out_ref, act_ref):
     step = pl.program_id(0)
 
     @pl.when(step < steps)
     def _():
         wide = dot(rows_ref[...], w1_ref[...])
-        cols = pl.ds(pl.multiple_of(step * ACT_COLS, ACT_COLS), ACT_COLS)
+        cols = pl.ds(pl.multiple_of(step * act_cols, act_cols), act_cols)
         act_ref[:, cols] = (wide * jax.nn.sigmoid(wide) * dot(rows_ref[...], w3_ref[...])).astype(BF16)
 
     @pl.when(step >= steps)
@@ -348,7 +435,7 @@
             return call(
                 functools.partial(down_kernel, (q_rank, kv_rank, rope, steps)), (steps + 1,), info,
                 [(flat_x, pl.BlockSpec((seq, width), lambda n, s: (s[1], 0))), (norm_attn, fixed(1, width)),
-                 (wq_down, pl.BlockSpec((width, DOWN_COLS), lambda n, s: (0, jnp.minimum(n, steps - 1)))), (norm_q, fixed(1, q_rank)),
+                 (wq_down, pl.BlockSpec((width, DOWN_COLS), lambda n, s: (0, s[0] * jnp.minimum(n, steps - 1)))), (norm_q, fixed(1, q_rank)),
                  (wkv_down, ANY), (norm_kv, fixed(1, kv_rank)), (cos_t, fixed(seq, rope)), (sin_t, fixed(seq, rope)), (token, ANY)],
                 [(((seq, joined_cols), BF16), fixed(seq, joined_cols)), (TOKEN, fixed(8, 128))],
                 [pltpu.VMEM((seq, width), BF16), pltpu.VMEM((seq, q_rank), BF16), pltpu.VMEM(wkv_down.shape, BF16), pltpu.SemaphoreType.DMA],
@@ -363,37 +450,41 @@
             out = (((seq, width), BF16), pl.BlockSpec((seq, OUT_COLS), lambda n, s: (0, later(n))))
             return call(
                 functools.partial(attention_kernel, (q_rank, kv_rank, nope, rope, v_head, steps)), (steps + width // OUT_COLS,), info,
-                [(own, ANY), (other, ANY), (wq_up, pl.BlockSpec((q_rank, q_cols), lambda n, s: (0, first(n)))),
-                 (wkv_up, pl.BlockSpec((kv_rank, kv_cols), lambda n, s: (0, first(n)))),
-                 (wo_part, pl.BlockSpec((heads * v_head, OUT_COLS), lambda n, s: (0, later(n)))),
+                [(own, ANY), (other, ANY), (wq_up, pl.BlockSpec((q_rank, q_cols), lambda n, s: (0, s[0] * first(n)))),
+                 (wkv_up, pl.BlockSpec((kv_rank, kv_cols), lambda n, s: (0, s[0] * first(n)))),
+                 (wo_part, pl.BlockSpec((heads * v_head, OUT_COLS), lambda n, s: (0, s[0] * later(n)))),
                  (cos_t, fixed(seq, rope)), (sin_t, fixed(seq, rope)), (token, ANY)],
                 [out, out, (TOKEN, fixed(8, 128))],
-                [pltpu.VMEM((2, seq, joined_cols), BF16), pltpu.VMEM((2, seq, heads * v_head), BF16), pltpu.SemaphoreType.DMA((2,))],
+                [pltpu.VMEM((2, seq, joined_cols), BF16), pltpu.VMEM((2, seq, q_cols), BF16), pltpu.VMEM((2, seq, kv_cols), BF16),
+                 pltpu.VMEM((seq, seq), F32), pltpu.VMEM((2, seq, seq), F32), pltpu.VMEM((2, seq, seq), BF16), pltpu.VMEM((2, seq, heads * v_head), BF16),
+                 pltpu.SemaphoreType.DMA((2,))],
                 2 * 2 * seq * (q_rank * wq_up.shape[1] + kv_rank * wkv_up.shape[1] + heads * v_head * width + heads * 3 * v_head * seq),
                 2 * (wq_up.size + wkv_up.size + wo_part.size + 2 * seq * width))
 
         def mlp(pieces, token):
-            steps = hidden_cols // ACT_COLS
+            steps, count = hidden_cols // ACT_COLS, len(pieces)
+            rows = count * half
             first = lambda n: jnp.minimum(n, steps - 1)
             later = lambda n: jnp.maximum(n - steps, 0)
-            out = (((seq, width), BF16), pl.BlockSpec((seq, OUT_COLS), lambda n, s: (0, later(n))))
+            out = (((rows // 2, width), BF16), pl.BlockSpec((rows // 2, OUT_COLS), lambda n, s: (0, later(n))))
             return call(
-                functools.partial(mlp_kernel, steps), (steps + width // OUT_COLS,), jnp.stack([active, active]),
+                functools.partial(mlp_kernel, steps, count), (steps + width // OUT_COLS,), jnp.stack([active, active]),
                 [(m, ANY) for m in pieces] + [
-                    (w1_part, pl.BlockSpec((width, ACT_COLS), lambda n, s: (0, first(n)))),
-                    (w3_part, pl.BlockSpec((width, ACT_COLS), lambda n, s: (0, first(n)))),
-                    (w2_part, pl.BlockSpec((hidden_cols, OUT_COLS), lambda n, s: (0, later(n)))), (token, ANY)],
+                    (w1_part, pl.BlockSpec((width, ACT_COLS), lambda n, s: (0, s[0] * first(n)))),
+                    (w3_part, pl.BlockSpec((width, ACT_COLS), lambda n, s: (0, s[0] * first(n)))),
+                    (w2_part, pl.BlockSpec((hidden_cols, OUT_COLS), lambda n, s: (0, s[0] * later(n)))), (token, ANY)],
                 [out, out, (TOKEN, fixed(8, 128))],
-                [pltpu.VMEM((2 * seq, width), BF16), pltpu.VMEM((2 * seq, hidden_cols), BF16), pltpu.SemaphoreType.DMA((4,))],
-                2 * 2 * seq * width * hidden_cols * 3, 2 * (3 * width * hidden_cols + 4 * seq * width))
+                [pltpu.VMEM((rows, width), BF16), pltpu.VMEM((rows, hidden_cols), BF16), pltpu.SemaphoreType.DMA((count,))],
+                2 * rows * width * hidden_cols * 3, 2 * (3 * width * hidden_cols + 2 * rows * width))
 
         ROW_STEP = 64
         low_rows = pl.BlockSpec((ROW_STEP, width), lambda n, s: (n, 0))
         high_rows = pl.BlockSpec((ROW_STEP, width), lambda n, s: (half // ROW_STEP + n, 0))
 
         def half_sum(near, other, token):
+            spec = high_rows if near.shape[0] > half else low_rows
             return call(add_kernel, (half // ROW_STEP,), jnp.stack([active]),
-                        [(near, high_rows), (other, high_rows), (token, ANY)],
+                        [(near, spec), (other, spec), (token, ANY)],
                         [(((half, width), BF16), low_rows), (TOKEN, fixed(8, 128))], [], half * width, 6 * half * width)
 
         def residual(i, near, other, from_chip, token):
@@ -406,45 +497,48 @@
 
         def next_latent(i, hidden, near, other, from_chip, token):
             mine = lax.slice_in_dim(seq_len, 2 * i, 2 * i + 2)
-            info = jnp.stack([chip * (half // ROWS), chip, jnp.where(core == 0, mine[0], mine[1])])
-            table = pl.BlockSpec((ROWS, rope), lambda n, s: (s[0] + n, 0))
-            low = pl.BlockSpec((ROWS, width), lambda n, s: (n, 0))
-            return call(functools.partial(next_kernel, scale, kv_rank), (half // ROWS,), info,
+            info = jnp.stack([chip, chip, jnp.where(core == 0, mine[0], mine[1]), active])
+            steps = half // ROW_STEP
+            table = pl.BlockSpec((half, rope), lambda n, s: (s[0], 0))
+            low = pl.BlockSpec((ROW_STEP, width), lambda n, s: (s[3] * jnp.minimum(n, steps - 1), 0))
+            return call(functools.partial(next_kernel, scale, kv_rank, steps), (steps + 1,), info,
                         [(hidden, low), (near, low), (other, low), (from_chip, low), (next_g_attn, fixed(1, width)),
-                         (next_wkv, fixed(*next_wkv.shape)), (next_g_kv, fixed(1, kv_rank)), (cos_t, table), (sin_t, table), (token, ANY)],
+                         (next_wkv, ANY), (next_g_kv, fixed(1, kv_rank)), (cos_t, table), (sin_t, table), (token, ANY)],
                         [(((half + 16, msg_cols), BF16), fixed(half + 16, msg_cols)), (TOKEN, fixed(8, 128))],
-                        [pltpu.VMEM((8, width), F32)], 2 * half * width * (kv_rank + rope), 8 * half * width + 2 * next_wkv.size)
+                        [pltpu.VMEM((half, width), BF16), pltpu.VMEM((half, width), BF16), pltpu.VMEM(next_wkv.shape, BF16),
+                         pltpu.SemaphoreType.DMA], 2 * half * width * (kv_rank + rope), 8 * half * width + 2 * next_wkv.size)
 
         def last_attention(lens, latent, rows):
             normed = rms_norm(rows, norm_attn[0])
             q_full = dot(rms_norm(dot(normed, wq_down).astype(BF16), norm_q[0]), wq_up).astype(BF16).reshape(2, heads, nope + rope)
             at = lens - 1
             q_full = jnp.concatenate([q_full[..., :nope], apply_rope(q_full[..., nope:], cos_t[at][:, None], sin_t[at][:, None])], axis=-1)
-            q_full = jnp.broadcast_to(q_full[:, :, None], (2, heads, 16, nope + rope))
+            q_full = jnp.broadcast_to(q_full[:, :, None], (2, heads, 8, nope + rope))
             info = jnp.concatenate([jnp.zeros((2,), jnp.int32), lens])
             blocks = heads // HEAD_BLOCK
             outs = call(functools.partial(last_kernel, (kv_rank, nope, rope, v_head)), (blocks,), info,
-                        [(q_full, pl.BlockSpec((2, HEAD_BLOCK, 16, nope + rope), lambda n, s: (0, n, 0, 0))), (latent, fixed(2, seq, msg_cols)),
+                        [(q_full, pl.BlockSpec((2, HEAD_BLOCK, 8, nope + rope), lambda n, s: (0, n, 0, 0))), (latent, fixed(2, seq, msg_cols)),
                          (wkv_up, pl.BlockSpec((kv_rank, HEAD_BLOCK * (nope + v_head)), lambda n, s: (0, n)))],
-                        [(((2, 16, heads * v_head), BF16), pl.BlockSpec((2, 16, HEAD_BLOCK * v_head), lambda n, s: (0, 0, n)))],
+                        [(((2, 8, heads * v_head), BF16), pl.BlockSpec((2, 8, HEAD_BLOCK * v_head), lambda n, s: (0, 0, n)))],
                         [], 4 * seq * kv_rank * wkv_up.shape[1], 2 * wkv_up.size)[0]
             return outs[:, 0]
 
         def rows_matmul(rows, weight):
             count, depth = rows.shape
-            return call(rows_kernel, (width // OUT_COLS,), jnp.stack([active]),
-                        [(rows, fixed(count, depth)), (weight, pl.BlockSpec((depth, OUT_COLS), lambda n, s: (0, n)))],
-                        [(((count, width), BF16), pl.BlockSpec((count, OUT_COLS), lambda n, s: (0, n)))],
+            cols = 2 * OUT_COLS
+            return call(rows_kernel, (width // cols,), jnp.stack([active]),
+                        [(rows, fixed(count, depth)), (weight, pl.BlockSpec((depth, cols), lambda n, s: (0, n)))],
+                        [(((count, width), BF16), pl.BlockSpec((count, cols), lambda n, s: (0, n)))],
                         [], 2 * count * weight.size, 2 * weight.size)[0]
 
         def rows_mlp(rows):
-            count = rows.shape[0]
-            steps = hidden_cols // ACT_COLS
+            count, act_cols = rows.shape[0], 2 * ACT_COLS
+            steps = hidden_cols // act_cols
             first = lambda n: jnp.minimum(n, steps - 1)
             later = lambda n: jnp.maximum(n - steps, 0)
-            return call(functools.partial(rows_mlp_kernel, steps), (steps + width // OUT_COLS,), jnp.stack([active]),
-                        [(rows, fixed(count, width)), (w1_part, pl.BlockSpec((width, ACT_COLS), lambda n, s: (0, first(n)))),
-                         (w3_part, pl.BlockSpec((width, ACT_COLS), lambda n, s: (0, first(n)))),
+            return call(functools.partial(rows_mlp_kernel, steps, act_cols), (steps + width // OUT_COLS,), jnp.stack([active]),
+                        [(rows, fixed(count, width)), (w1_part, pl.BlockSpec((width, act_cols), lambda n, s: (0, first(n)))),
+                         (w3_part, pl.BlockSpec((width, act_cols), lambda n, s: (0, first(n)))),
                          (w2_part, pl.BlockSpec((hidden_cols, OUT_COLS), lambda n, s: (0, later(n))))],
                         [(((count, width), BF16), pl.BlockSpec((count, OUT_COLS), lambda n, s: (0, later(n))))],
                         [pltpu.VMEM((count, hidden_cols), BF16)], 6 * count * w1_part.size, 6 * w1_part.size)[0]
@@ -483,6 +577,18 @@
         def run_mlp(i):
             nonlocal token
             near, far, token = mlp(state[i]["pieces"], token)
+            state[i].update(near=near, from_core=swap(far, "core", 0))
+
+        def run_mlpx(i):
+            nonlocal token
+            pieces = state[i]["pieces"]
+            near, far, token = mlp((pieces[1], pieces[3]), token)
+            state[i].update(near=near, from_core=swap(far, "core", 0))
+
+        def run_mlpo(i):
+            nonlocal token
+            pieces = state[i]["pieces"]
+            near, far, token = mlp((pieces[0], pieces[2]), token)
             state[i].update(near=near, from_core=swap(far, "core", 0))
 
         def run_next(i):
@@ -509,7 +615,7 @@
             return (jnp.zeros((2, heads * v_head), BF16), jnp.zeros((2, width), BF16),
                     cut(q_rank, q_rank + kv_rank), cut(q_rank + kv_rank, q_rank + kv_rank + rope))
 
-        run = dict(down=run_down, att=run_att, suma=run_suma, res=run_res, mlp=run_mlp, summ=run_summ, next=run_next)
+        run = dict(mlpx=run_mlpx, mlpo=run_mlpo, down=run_down, att=run_att, suma=run_suma, res=run_res, mlp=run_mlp, summ=run_summ, next=run_next)
         for kind, i in ORDER:
             run[kind](i)
         ends = []

time: 1970 us -> 1790 us (0.909)
  Pallas kernels: 1180 us -> 1070 us
  waiting for transfers between devices: 611 us -> 549 us
    pallas_call x30 -> x31, Pallas kernels: 1180 us -> 1070 us  [call(): pl.pallas_call(kernel, grid_spec=pltpu.PrefetchScalarGridSpec(num_scalar_...]
    ppermute x1, waiting for transfers between devices: 170 us -> 139 us  [program(): lax.ppermute(final, 'pp', up)]
    ppermute x48 -> x49, waiting for transfers between devices: 422 us -> 392 us  [swap(): lax.ppermute(value, ('pp', axis), [(2 * stage_of, 2 * stage_of + 1), (2 *...]
    ppermute x48 -> x49, starting transfers between devices: 96.1 us -> 96.7 us  [swap(): lax.ppermute(value, ('pp', axis), [(2 * stage_of, 2 * stage_of + 1), (2 *...]
  transfers between devices with their start and end apart: 56 -> 57, of which waited for: 13 -> 13; matrix products, arithmetic and copies ran while one was open for 1% -> 1% of each run, Pallas kernels for 40% -> 44%
where the time goes in v2:
time: 1790 us; the launch traced here: 1780 us
  Pallas kernels  1070 us (60%)
  waiting for transfers between devices  549 us (31%)
  starting transfers between devices  115 us (6%)
  other arithmetic  19.8 us (1%)
    pallas_call x31, Pallas kernels, call(): pl.pallas_call(kernel, grid_spec=pltpu.PrefetchScalarGridSpec(num_scalar_...  1070 us
    ppermute x49, waiting for transfers between devices, swap(): lax.ppermute(value, ('pp', axis), [(2 * stage_of, 2 * stage_of + 1), (2 *...  392 us
    ppermute x1, waiting for transfers between devices, program(): lax.ppermute(final, 'pp', up)  139 us
    ppermute x49, starting transfers between devices, swap(): lax.ppermute(value, ('pp', axis), [(2 * stage_of, 2 * stage_of + 1), (2 *...  96.7 us
  transfers between devices with their start and end apart: 57, of which 13 were waited for; matrix products, arithmetic and copies ran while one was open for 1% of the time, Pallas kernels for 44%

profile of v2, /device:TPU:0, one launch (start us, length us, event | category | flops | bytes accessed | tf_op | source)
XLA Modules:
  0.0 1780.2 jit_solution(17430931920864873351)
XLA Ops:
  1.9 25.0 %shard_map.184 = (bf16[512,2176]{1,0:T(8,128)(2,1)}, f32[8,128]{1,0:T(8,128)}) custom-call(s32[2]{0:T(128)} %get-tuple-element.466.info, bf16[4096,6144]{1,0:T(8,128)(2,1)} %bitcast.138, bf16[1,6144]{1,0:T(2,128)(2,1)} %g_attn.7, bf16[6144,1536]{1,0:T(8,128)(2,1)} %bitcast.146, bf16[1,1536]{1,0:T(2,128)(2,1)} %g_q.7, bf16[576,6144]{1,0:T(8,128)(2,1)} %bitcast.170, ...), custom_call_target="tpu_custom_call" | custom-call | flops 13287555072 | bytes 33030144 | tf_op jit(solution)/shard_map/pallas_call | solution.py:71
  42.2 23.2 %shard_map.185 = (bf16[512,2176]{1,0:T(8,128)(2,1)S(1)}, f32[8,128]{1,0:T(8,128)}) custom-call(s32[2]{0:T(128)} %get-tuple-element.467.info, bf16[4096,6144]{1,0:T(8,128)(2,1)} %bitcast.139, bf16[1,6144]{1,0:T(2,128)(2,1)S(1)} %copy-done.10, bf16[6144,1536]{1,0:T(8,128)(2,1)} %bitcast.147, bf16[1,1536]{1,0:T(2,128)(2,1)S(1)} %copy-done.16, ...), custom_call_target="tpu_custom_call" | custom-call | flops 13287555072 | bytes 33030144 | tf_op jit(solution)/shard_map/pallas_call | solution.py:71
  65.5 64.7 %shard_map.186 = (bf16[512,6144]{1,0:T(8,128)(2,1)}, bf16[512,6144]{1,0:T(8,128)(2,1)}, f32[8,128]{1,0:T(8,128)}) custom-call(s32[4]{0:T(128)} %get-tuple-element.457.info, bf16[512,2176]{1,0:T(8,128)(2,1)} %get-tuple-element.297.own_hbm, bf16[512,2176]{1,0:T(8,128)(2,1)} %collective-permute-done.other_hbm, bf16[1536,3072]{1,0:T(8,128)(2,1)} %bitcast.154, ...), custom_call_target="tpu_custom_call" | custom-call | flops 46170898432 | bytes 51380224 | tf_op jit(solution)/shard_map/pallas_call | solution.py:71
  135.1 24.1 %shard_map.187 = (bf16[512,2176]{1,0:T(8,128)(2,1)}, f32[8,128]{1,0:T(8,128)}) custom-call(s32[2]{0:T(128)} %pad_add_fusion.5.info, bf16[4096,6144]{1,0:T(8,128)(2,1)} %bitcast.140, bf16[1,6144]{1,0:T(2,128)(2,1)S(1)} %copy-done.10, bf16[6144,1536]{1,0:T(8,128)(2,1)} %bitcast.148, bf16[1,1536]{1,0:T(2,128)(2,1)S(1)} %copy-done.16, ...), custom_call_target="tpu_custom_call" | custom-call | flops 13287555072 | bytes 33030144 | tf_op jit(solution)/shard_map/pallas_call | solution.py:71
  164.3 63.4 %shard_map.189 = (bf16[512,6144]{1,0:T(8,128)(2,1)}, bf16[512,6144]{1,0:T(8,128)(2,1)}, f32[8,128]{1,0:T(8,128)}) custom-call(s32[4]{0:T(128)} %get-tuple-element.456.info, bf16[512,2176]{1,0:T(8,128)(2,1)S(1)} %get-tuple-element.305.own_hbm, bf16[512,2176]{1,0:T(8,128)(2,1)} %collective-permute-done.3.other_hbm, bf16[1536,3072]{1,0:T(8,128)(2,1)} %bitcast.155, ...), custom_call_target="tpu_custom_call" | custom-call | flops 46170898432 | bytes 51380224 | tf_op jit(solution)/shard_map/pallas_call | solution.py:71
  237.0 23.2 %shard_map.190 = (bf16[512,2176]{1,0:T(8,128)(2,1)S(1)}, f32[8,128]{1,0:T(8,128)}) custom-call(s32[2]{0:T(128)} %pad_add_fusion.7.info, bf16[4096,6144]{1,0:T(8,128)(2,1)} %bitcast.141, bf16[1,6144]{1,0:T(2,128)(2,1)S(1)} %copy-done.10, bf16[6144,1536]{1,0:T(8,128)(2,1)} %bitcast.149, bf16[1,1536]{1,0:T(2,128)(2,1)S(1)} %copy-done.16, ...), custom_call_target="tpu_custom_call" | custom-call | flops 13287555072 | bytes 33030144 | tf_op jit(solution)/shard_map/pallas_call | solution.py:71
  269.7 34.0 %collective-permute-done.2.chip_ref = bf16[256,6144]{1,0:T(8,128)(2,1)} collective-permute-done((bf16[256,6144]{1,0:T(8,128)(2,1)}, bf16[256,6144]{1,0:T(8,128)(2,1)}, u32[]{:S(2)}, u32[]{:S(2)}) %collective-permute-start.2) | collective-permute-done | bytes 3145760 | tf_op jit(solution)/shard_map/ppermute | solution.py:550
  316.2 64.2 %shard_map.193 = (bf16[512,6144]{1,0:T(8,128)(2,1)}, bf16[512,6144]{1,0:T(8,128)(2,1)}, f32[8,128]{1,0:T(8,128)}) custom-call(s32[4]{0:T(128)} %get-tuple-element.397.info, bf16[512,2176]{1,0:T(8,128)(2,1)} %get-tuple-element.314.own_hbm, bf16[512,2176]{1,0:T(8,128)(2,1)} %collective-permute-done.8.other_hbm, bf16[1536,3072]{1,0:T(8,128)(2,1)} %bitcast.156, ...), custom_call_target="tpu_custom_call" | custom-call | flops 46170898432 | bytes 51380224 | tf_op jit(solution)/shard_map/pallas_call | solution.py:71
  397.9 40.6 %collective-permute-done.5.refs_1_ = bf16[256,6144]{1,0:T(8,128)(2,1)} collective-permute-done((bf16[256,6144]{1,0:T(8,128)(2,1)}, bf16[256,6144]{1,0:T(8,128)(2,1)}, u32[]{:S(2)}, u32[]{:S(2)}) %collective-permute-start.5) | collective-permute-done | bytes 3145760 | tf_op jit(solution)/shard_map/ppermute | solution.py:550
  440.4 63.3 %shard_map.195 = (bf16[512,6144]{1,0:T(8,128)(2,1)}, bf16[512,6144]{1,0:T(8,128)(2,1)}, f32[8,128]{1,0:T(8,128)}) custom-call(s32[4]{0:T(128)} %get-tuple-element.455.info, bf16[512,2176]{1,0:T(8,128)(2,1)S(1)} %get-tuple-element.318.own_hbm, bf16[512,2176]{1,0:T(8,128)(2,1)} %collective-permute-done.10.other_hbm, bf16[1536,3072]{1,0:T(8,128)(2,1)} %bitcast.157, ...), custom_call_target="tpu_custom_call" | custom-call | flops 46170898432 | bytes 51380224 | tf_op jit(solution)/shard_map/pallas_call | solution.py:71
  517.2 131.6 %shard_map.197 = (bf16[512,6144]{1,0:T(8,128)(2,1)}, bf16[512,6144]{1,0:T(8,128)(2,1)}, f32[8,128]{1,0:T(8,128)}) custom-call(s32[2]{0:T(128)} %pad_add_fusion.8.info, bf16[256,6144]{1,0:T(8,128)(2,1)} %get-tuple-element.313.refs_0_, bf16[256,6144]{1,0:T(8,128)(2,1)} %collective-permute-done.5.refs_1_, bf16[256,6144]{1,0:T(8,128)(2,1)} %collective-permute-done.6.refs_2_, ...), custom_call_target="tpu_custom_call" | custom-call | flops 115964116992 | bytes 138412032 | tf_op jit(solution)/shard_map/pallas_call | solution.py:71
  666.6 131.3 %shard_map.200 = (bf16[512,6144]{1,0:T(8,128)(2,1)}, bf16[512,6144]{1,0:T(8,128)(2,1)}, f32[8,128]{1,0:T(8,128)}) custom-call(s32[2]{0:T(128)} %pad_add_fusion.8.info, bf16[256,6144]{1,0:T(8,128)(2,1)} %get-tuple-element.326.refs_0_, bf16[256,6144]{1,0:T(8,128)(2,1)} %collective-permute-done.13.refs_1_, bf16[256,6144]{1,0:T(8,128)(2,1)} %collective-permute-done.14.refs_2_, ...), custom_call_target="tpu_custom_call" | custom-call | flops 115964116992 | bytes 138412032 | tf_op jit(solution)/shard_map/pallas_call | solution.py:71
  807.6 65.4 %collective-permute-done.22.refs_1_ = bf16[256,6144]{1,0:T(8,128)(2,1)} collective-permute-done((bf16[256,6144]{1,0:T(8,128)(2,1)}, bf16[256,6144]{1,0:T(8,128)(2,1)}, u32[]{:S(2)}, u32[]{:S(2)}) %collective-permute-start.22) | collective-permute-done | bytes 3145760 | tf_op jit(solution)/shard_map/ppermute | solution.py:550
  881.4 58.5 %collective-permute-done.26.chip_ref = bf16[256,6144]{1,0:T(8,128)(2,1)S(1)} collective-permute-done((bf16[256,6144]{1,0:T(8,128)(2,1)}, bf16[256,6144]{1,0:T(8,128)(2,1)S(1)}, u32[]{:S(2)}, u32[]{:S(2)}) %collective-permute-start.26) | collective-permute-done | bytes 3145760 | tf_op jit(solution)/shard_map/ppermute | solution.py:550
  955.5 131.7 %shard_map.204 = (bf16[512,6144]{1,0:T(8,128)(2,1)}, bf16[512,6144]{1,0:T(8,128)(2,1)}, f32[8,128]{1,0:T(8,128)}) custom-call(s32[2]{0:T(128)} %pad_add_fusion.8.info, bf16[256,6144]{1,0:T(8,128)(2,1)} %get-tuple-element.335.refs_0_, bf16[256,6144]{1,0:T(8,128)(2,1)} %collective-permute-done.22.refs_1_, bf16[256,6144]{1,0:T(8,128)(2,1)} %collective-permute-done.23.refs_2_, ...), custom_call_target="tpu_custom_call" | custom-call | flops 115964116992 | bytes 138412032 | tf_op jit(solution)/shard_map/pallas_call | solution.py:71
  1095.0 67.3 %collective-permute-done.32.refs_0_ = bf16[256,6144]{1,0:T(8,128)(2,1)} collective-permute-done((bf16[256,6144]{1,0:T(8,128)(2,1)}, bf16[256,6144]{1,0:T(8,128)(2,1)}, u32[]{:S(2)}, u32[]{:S(2)}) %collective-permute-start.32) | collective-permute-done | bytes 3145760 | tf_op jit(solution)/shard_map/ppermute | solution.py:550
  1177.7 52.1 %collective-permute-done.18.chip_ref = bf16[256,6144]{1,0:T(8,128)(2,1)} collective-permute-done((bf16[256,6144]{1,0:T(8,128)(2,1)}, bf16[256,6144]{1,0:T(8,128)(2,1)}, u32[]{:S(2)}, u32[]{:S(2)}) %collective-permute-start.18) | collective-permute-done | bytes 3145760 | tf_op jit(solution)/shard_map/ppermute | solution.py:550
  1249.3 72.2 %shard_map.207 = (bf16[256,6144]{1,0:T(8,128)(2,1)}, bf16[256,6144]{1,0:T(8,128)(2,1)}, f32[8,128]{1,0:T(8,128)}) custom-call(s32[2]{0:T(128)} %pad_add_fusion.8.info, bf16[256,6144]{1,0:T(8,128)(2,1)} %collective-permute-done.32.refs_0_, bf16[256,6144]{1,0:T(8,128)(2,1)} %collective-permute-done.33.refs_1_, bf16[6144,3072]{1,0:T(8,128)(2,1)} %bitcast.178, ...), custom_call_target="tpu_custom_call" | custom-call | flops 57982058496 | bytes 125829120 | tf_op jit(solution)/shard_map/pallas_call | solution.py:71
  1339.3 24.9 %collective-permute-done.39.chip_ref = bf16[256,6144]{1,0:T(8,128)(2,1)} collective-permute-done((bf16[256,6144]{1,0:T(8,128)(2,1)}, bf16[256,6144]{1,0:T(8,128)(2,1)}, u32[]{:S(2)}, u32[]{:S(2)}) %collective-permute-start.39) | collective-permute-done | bytes 3145760 | tf_op jit(solution)/shard_map/ppermute | solution.py:550
  1381.5 72.5 %shard_map.211 = (bf16[256,6144]{1,0:T(8,128)(2,1)}, bf16[256,6144]{1,0:T(8,128)(2,1)}, f32[8,128]{1,0:T(8,128)}) custom-call(s32[2]{0:T(128)} %pad_add_fusion.8.info, bf16[256,6144]{1,0:T(8,128)(2,1)} %get-tuple-element.347.refs_0_, bf16[256,6144]{1,0:T(8,128)(2,1)} %collective-permute-done.44.refs_1_, bf16[6144,3072]{1,0:T(8,128)(2,1)} %bitcast.179, ...), custom_call_target="tpu_custom_call" | custom-call | flops 57982058496 | bytes 125829120 | tf_op jit(solution)/shard_map/pallas_call | solution.py:71
  1479.6 49.1 %collective-permute-done.47.chip_ref = bf16[256,6144]{1,0:T(8,128)(2,1)} collective-permute-done((bf16[256,6144]{1,0:T(8,128)(2,1)}, bf16[256,6144]{1,0:T(8,128)(2,1)}, u32[]{:S(2)}, u32[]{:S(2)}) %collective-permute-start.47) | collective-permute-done | bytes 3145760 | tf_op jit(solution)/shard_map/ppermute | solution.py:550
  1528.7 12.3 shard_map.212
  1589.9 42.3 %shard_map.214 = bf16[8,6144]{1,0:T(8,128)(2,1)} custom-call(s32[1]{0:T(128)} %bitcast.44.info, bf16[8,6144]{1,0:T(8,128)(2,1)} %fusion.45.rows_ref, bf16[6144,3072]{1,0:T(8,128)(2,1)} %bitcast.180, bf16[6144,3072]{1,0:T(8,128)(2,1)} %bitcast.186, bf16[3072,6144]{1,0:T(8,128)(2,1)} %bitcast.192), custom_call_target="tpu_custom_call" | custom-call | flops 905969664 | bytes 113246208 | tf_op jit(solution)/shard_map/pallas_call | solution.py:71
  1640.6 138.8 %collective-permute-done.56 = bf16[8,6144]{1,0:T(8,128)(2,1)S(1)} collective-permute-done((bf16[8,6144]{1,0:T(8,128)(2,1)S(1)}, bf16[8,6144]{1,0:T(8,128)(2,1)S(1)}, u32[]{:S(2)}, u32[]{:S(2)}) %collective-permute-start.56) | collective-permute-done | bytes 98336 | tf_op jit(solution)/shard_map/ppermute | solution.py:636
  (239 shorter events, 306.2 us)
Async XLA Ops:
  234.4 81.8 %collective-permute-start.8 = (bf16[512,2176]{1,0:T(8,128)(2,1)}, bf16[512,2176]{1,0:T(8,128)(2,1)}, u32[]{:S(2)}, u32[]{:S(2)}) collective-permute-start(bf16[512,2176]{1,0:T(8,128)(2,1)} %get-tuple-element.314.own_hbm), channel_id=1, source_target_pairs={{0,1},{1,0},{2,3},{3,2}} | collective-permute-start | bytes 6684680 | tf_op jit(solution)/shard_map/ppermute | solution.py:550
  260.2 135.8 %collective-permute-start.10 = (bf16[512,2176]{1,0:T(8,128)(2,1)S(1)}, bf16[512,2176]{1,0:T(8,128)(2,1)}, u32[]{:S(2)}, u32[]{:S(2)}) collective-permute-start(bf16[512,2176]{1,0:T(8,128)(2,1)S(1)} %get-tuple-element.318.own_hbm), channel_id=1, source_target_pairs={{0,1},{1,0},{2,3},{3,2}} | collective-permute-start | bytes 6684680 | tf_op jit(solution)/shard_map/ppermute | solution.py:550
  267.8 117.6 %collective-permute-start.11 = (bf16[256,6144]{1,0:T(8,128)(2,1)}, bf16[256,6144]{1,0:T(8,128)(2,1)}, u32[]{:S(2)}, u32[]{:S(2)}) collective-permute-start(bf16[256,6144]{1,0:T(8,128)(2,1)} %get-tuple-element.319), channel_id=1, source_target_pairs={{0,2},{2,0},{1,3},{3,1}} | collective-permute-start | bytes 9437192 | tf_op jit(solution)/shard_map/ppermute | solution.py:550
  312.3 126.3 %collective-permute-start.5 = (bf16[256,6144]{1,0:T(8,128)(2,1)}, bf16[256,6144]{1,0:T(8,128)(2,1)}, u32[]{:S(2)}, u32[]{:S(2)}) collective-permute-start(bf16[256,6144]{1,0:T(8,128)(2,1)} %get-tuple-element.313.refs_0_), channel_id=1, source_target_pairs={{0,2},{2,0},{1,3},{3,1}} | collective-permute-start | bytes 9437192 | tf_op jit(solution)/shard_map/ppermute | solution.py:550
  380.4 123.3 %collective-permute-start.9 = (bf16[512,6144]{1,0:T(8,128)(2,1)}, bf16[512,6144]{1,0:T(8,128)(2,1)}, u32[]{:S(2)}, u32[]{:S(2)}) collective-permute-start(bf16[512,6144]{1,0:T(8,128)(2,1)} %get-tuple-element.317), channel_id=1, source_target_pairs={{0,1},{1,0},{2,3},{3,2}} | collective-permute-start | bytes 18874376 | tf_op jit(solution)/shard_map/ppermute | solution.py:550
  383.0 128.3 %collective-permute-start.6 = (bf16[256,6144]{1,0:T(8,128)(2,1)}, bf16[256,6144]{1,0:T(8,128)(2,1)}, u32[]{:S(2)}, u32[]{:S(2)}) collective-permute-start(bf16[256,6144]{1,0:T(8,128)(2,1)} %get-tuple-element.313.refs_0_), channel_id=1, source_target_pairs={{0,1},{1,0},{2,3},{3,2}} | collective-permute-start | bytes 9437192 | tf_op jit(solution)/shard_map/ppermute | solution.py:550
  394.0 121.2 %collective-permute-start.13 = (bf16[256,6144]{1,0:T(8,128)(2,1)}, bf16[256,6144]{1,0:T(8,128)(2,1)}, u32[]{:S(2)}, u32[]{:S(2)}) collective-permute-start(bf16[256,6144]{1,0:T(8,128)(2,1)} %get-tuple-element.326.refs_0_), channel_id=1, source_target_pairs={{0,2},{2,0},{1,3},{3,1}} | collective-permute-start | bytes 9437192 | tf_op jit(solution)/shard_map/ppermute | solution.py:550
  396.0 270.6 %collective-permute-start.14 = (bf16[256,6144]{1,0:T(8,128)(2,1)}, bf16[256,6144]{1,0:T(8,128)(2,1)}, u32[]{:S(2)}, u32[]{:S(2)}) collective-permute-start(bf16[256,6144]{1,0:T(8,128)(2,1)} %get-tuple-element.326.refs_0_), channel_id=1, source_target_pairs={{0,1},{1,0},{2,3},{3,2}} | collective-permute-start | bytes 9437192 | tf_op jit(solution)/shard_map/ppermute | solution.py:550
  438.5 78.7 %collective-permute-start.7 = (bf16[256,6144]{1,0:T(8,128)(2,1)}, bf16[256,6144]{1,0:T(8,128)(2,1)}, u32[]{:S(2)}, u32[]{:S(2)}) collective-permute-start(bf16[256,6144]{1,0:T(8,128)(2,1)} %collective-permute-done.5.refs_1_), channel_id=1, source_target_pairs={{0,1},{1,0},{2,3},{3,2}} | collective-permute-start | bytes 9437192 | tf_op jit(solution)/shard_map/ppermute | solution.py:550
  503.7 157.7 %collective-permute-start.16 = (bf16[512,6144]{1,0:T(8,128)(2,1)}, bf16[512,6144]{1,0:T(8,128)(2,1)}, u32[]{:S(2)}, u32[]{:S(2)}) collective-permute-start(bf16[512,6144]{1,0:T(8,128)(2,1)} %get-tuple-element.328), channel_id=1, source_target_pairs={{0,1},{1,0},{2,3},{3,2}} | collective-permute-start | bytes 18874376 | tf_op jit(solution)/shard_map/ppermute | solution.py:550
  511.3 139.9 %collective-permute-start.17 = (bf16[256,6144]{1,0:T(8,128)(2,1)}, bf16[256,6144]{1,0:T(8,128)(2,1)S(1)}, u32[]{:S(2)}, u32[]{:S(2)}) collective-permute-start(bf16[256,6144]{1,0:T(8,128)(2,1)} %get-tuple-element.329), channel_id=1, source_target_pairs={{0,2},{2,0},{1,3},{3,1}} | collective-permute-start | bytes 9437192 | tf_op jit(solution)/shard_map/ppermute | solution.py:550
  515.2 151.4 %collective-permute-start.15 = (bf16[256,6144]{1,0:T(8,128)(2,1)}, bf16[256,6144]{1,0:T(8,128)(2,1)}, u32[]{:S(2)}, u32[]{:S(2)}) collective-permute-start(bf16[256,6144]{1,0:T(8,128)(2,1)} %collective-permute-done.13.refs_1_), channel_id=1, source_target_pairs={{0,1},{1,0},{2,3},{3,2}} | collective-permute-start | bytes 9437192 | tf_op jit(solution)/shard_map/ppermute | solution.py:550
  648.8 226.2 %collective-permute-start.12 = (bf16[512,6144]{1,0:T(8,128)(2,1)}, bf16[512,6144]{1,0:T(8,128)(2,1)}, u32[]{:S(2)}, u32[]{:S(2)}) collective-permute-start(bf16[512,6144]{1,0:T(8,128)(2,1)} %get-tuple-element.325), channel_id=1, source_target_pairs={{0,1},{1,0},{2,3},{3,2}} | collective-permute-start | bytes 18874376 | tf_op jit(solution)/shard_map/ppermute | solution.py:550
  797.9 152.4 %collective-permute-start.25 = (bf16[512,6144]{1,0:T(8,128)(2,1)}, bf16[512,6144]{1,0:T(8,128)(2,1)}, u32[]{:S(2)}, u32[]{:S(2)}) collective-permute-start(bf16[512,6144]{1,0:T(8,128)(2,1)} %get-tuple-element.337), channel_id=1, source_target_pairs={{0,1},{1,0},{2,3},{3,2}} | collective-permute-start | bytes 18874376 | tf_op jit(solution)/shard_map/ppermute | solution.py:550
  801.8 138.1 %collective-permute-start.26 = (bf16[256,6144]{1,0:T(8,128)(2,1)}, bf16[256,6144]{1,0:T(8,128)(2,1)S(1)}, u32[]{:S(2)}, u32[]{:S(2)}) collective-permute-start(bf16[256,6144]{1,0:T(8,128)(2,1)} %get-tuple-element.338), channel_id=1, source_target_pairs={{0,2},{2,0},{1,3},{3,1}} | collective-permute-start | bytes 9437192 | tf_op jit(solution)/shard_map/ppermute | solution.py:550
  805.7 149.8 %collective-permute-start.23 = (bf16[256,6144]{1,0:T(8,128)(2,1)}, bf16[256,6144]{1,0:T(8,128)(2,1)}, u32[]{:S(2)}, u32[]{:S(2)}) collective-permute-start(bf16[256,6144]{1,0:T(8,128)(2,1)} %get-tuple-element.335.refs_0_), channel_id=1, source_target_pairs={{0,1},{1,0},{2,3},{3,2}} | collective-permute-start | bytes 9437192 | tf_op jit(solution)/shard_map/ppermute | solution.py:550
  873.0 82.4 %collective-permute-start.24 = (bf16[256,6144]{1,0:T(8,128)(2,1)}, bf16[256,6144]{1,0:T(8,128)(2,1)}, u32[]{:S(2)}, u32[]{:S(2)}) collective-permute-start(bf16[256,6144]{1,0:T(8,128)(2,1)} %collective-permute-done.22.refs_1_), channel_id=1, source_target_pairs={{0,1},{1,0},{2,3},{3,2}} | collective-permute-start | bytes 9437192 | tf_op jit(solution)/shard_map/ppermute | solution.py:550
  875.0 302.7 %collective-permute-start.20 = (bf16[576,6144]{1,0:T(8,128)(2,1)}, bf16[576,6144]{1,0:T(8,128)(2,1)}, u32[]{:S(2)}, u32[]{:S(2)}) collective-permute-start(bf16[576,6144]{1,0:T(8,128)(2,1)} %bitcast.174), channel_id=1, source_target_pairs={{4,0},{5,1},{6,2},{7,3}} | collective-permute-start | bytes 21233672 | tf_op jit(solution)/shard_map/ppermute | solution.py:428
  1087.2 154.8 %collective-permute-start.34 = (bf16[512,6144]{1,0:T(8,128)(2,1)}, bf16[512,6144]{1,0:T(8,128)(2,1)}, u32[]{:S(2)}, u32[]{:S(2)}) collective-permute-start(bf16[512,6144]{1,0:T(8,128)(2,1)} %get-tuple-element.349), channel_id=1, source_target_pairs={{0,1},{1,0},{2,3},{3,2}} | collective-permute-start | bytes 18874376 | tf_op jit(solution)/shard_map/ppermute | solution.py:550
  1091.4 138.4 %collective-permute-start.18 = (bf16[256,6144]{1,0:T(8,128)(2,1)}, bf16[256,6144]{1,0:T(8,128)(2,1)}, u32[]{:S(2)}, u32[]{:S(2)}) collective-permute-start(bf16[256,6144]{1,0:T(8,128)(2,1)} %get-tuple-element.334), channel_id=1, source_target_pairs={{0,2},{2,0},{1,3},{3,1}} | collective-permute-start | bytes 9437192 | tf_op jit(solution)/shard_map/ppermute | solution.py:550
  1162.4 87.0 %collective-permute-start.33 = (bf16[256,6144]{1,0:T(8,128)(2,1)}, bf16[256,6144]{1,0:T(8,128)(2,1)}, u32[]{:S(2)}, u32[]{:S(2)}) collective-permute-start(bf16[256,6144]{1,0:T(8,128)(2,1)} %collective-permute-done.32.refs_0_), channel_id=1, source_target_pairs={{0,1},{1,0},{2,3},{3,2}} | collective-permute-start | bytes 9437192 | tf_op jit(solution)/shard_map/ppermute | solution.py:550
  1175.5 151.6 %collective-permute-start.31 = (bf16[256,6144]{1,0:T(8,128)(2,1)}, bf16[256,6144]{1,0:T(8,128)(2,1)}, u32[]{:S(2)}, u32[]{:S(2)}) collective-permute-start(bf16[256,6144]{1,0:T(8,128)(2,1)} %get-tuple-element.346), channel_id=1, source_target_pairs={{0,2},{2,0},{1,3},{3,1}} | collective-permute-start | bytes 9437192 | tf_op jit(solution)/shard_map/ppermute | solution.py:550
  1247.1 117.0 %collective-permute-start.39 = (bf16[256,6144]{1,0:T(8,128)(2,1)}, bf16[256,6144]{1,0:T(8,128)(2,1)}, u32[]{:S(2)}, u32[]{:S(2)}) collective-permute-start(bf16[256,6144]{1,0:T(8,128)(2,1)} %get-tuple-element.356), channel_id=1, source_target_pairs={{0,2},{2,0},{1,3},{3,1}} | collective-permute-start | bytes 9437192 | tf_op jit(solution)/shard_map/ppermute | solution.py:550
  1638.4 141.0 %collective-permute-start.56 = (bf16[8,6144]{1,0:T(8,128)(2,1)S(1)}, bf16[8,6144]{1,0:T(8,128)(2,1)S(1)}, u32[]{:S(2)}, u32[]{:S(2)}) collective-permute-start(bf16[8,6144]{1,0:T(8,128)(2,1)S(1)} %fusion.42), channel_id=1, source_target_pairs={{4,0},{5,1},{6,2},{7,3}} | collective-permute-start | bytes 294920 | tf_op jit(solution)/shard_map/ppermute | solution.py:636
  (63 other events, 2979.6 us)
